TPU v7x, 128 devices: a whole 4x4x4 slice. The times are simulated.
128 devices in a mesh: pod: 1, data: 64 (over z, y, x), model: 2 (over core).
Axes of the slice: x: 4, y: 4, z: 4, core: 2. Of those that a mesh axis runs over, the one named last changes fastest.
Arguments:
- x_in: bfloat16 [64, 1024, 2048], P(('pod', 'data'), 'model')
- dy_in: bfloat16 [64, 1024, 2048], P(('pod', 'data'), 'model')
- w_q: bfloat16 [2048, 8, 256], P(None, 'model')
- w_k: bfloat16 [1, 2048, 256], replicated
- w_v: bfloat16 [1, 2048, 256], replicated
- w_o: bfloat16 [8, 256, 2048], P('model')
Outputs:
- output 1: bfloat16 [64, 1024, 2048], P(('pod', 'data'), 'model')
- output 2: float32 [2048, 8, 256], P(('pod', 'data'), 'model')
- output 3: float32 [2048, 256], P(('pod', 'model', 'data'))
- output 4: float32 [2048, 256], P(('pod', 'model', 'data'))
- output 5: float32 [8, 256, 2048], P(('pod', 'model'), None, 'data')
All inputs are finite; a program needn't handle non-finite values.
Results may differ from a plain program's by a relative error of at most 0.0103.
Values are sent between devices in bfloat16 or wider.
A program may use at most 1 GiB of HBM per device.

v0:
```python
import jax
import jax.numpy as jnp
from jax import lax
from jax.sharding import PartitionSpec as P


def subgroup_pairs(step_shift, sub_size, axis_size):
    return [(start_dev + member, start_dev + (member + step_shift) % sub_size)
            for start_dev in range(0, axis_size, sub_size) for member in range(sub_size)]


def subgroup_scatter_sum(grad_parts, sub_size, axis_size):
    my_slot = lax.axis_index('model') % sub_size
    lead_dim, row_count, col_count = grad_parts.shape
    row_blocks = grad_parts.reshape(lead_dim, sub_size, row_count // sub_size, col_count)
    total_sum = lax.dynamic_index_in_dim(row_blocks, my_slot, axis=1, keepdims=False)
    for step_shift in range(1, sub_size):
        outgoing = lax.dynamic_index_in_dim(row_blocks, (my_slot + step_shift) % sub_size, axis=1, keepdims=False)
        total_sum = total_sum + lax.ppermute(outgoing, 'model', subgroup_pairs(step_shift, sub_size, axis_size))
    return total_sum


def solution(mesh):
    model_size = mesh.shape['model']
    tok_spec = P(('pod', 'data'), 'model', None)

    def device_step(x_loc, dy_loc, w_q, w_k, w_v, w_o):
        kv_heads = w_k.shape[0]
        head_dim = w_k.shape[2]
        sub_size = model_size // kv_heads
        score_scale = head_dim ** -0.5
        kv_index = lax.axis_index('model') // sub_size
        x_full = lax.all_gather(x_loc, 'model', axis=1, tiled=True)
        dy_full = lax.all_gather(dy_loc, 'model', axis=1, tiled=True)
        kv_weights = jnp.stack([lax.dynamic_index_in_dim(w_k, kv_index, axis=0, keepdims=False),
                                lax.dynamic_index_in_dim(w_v, kv_index, axis=0, keepdims=False)])
        seq_len = x_full.shape[1]
        causal = lax.broadcasted_iota(jnp.int32, (seq_len, seq_len), 0) >= lax.broadcasted_iota(jnp.int32, (seq_len, seq_len), 1)
        q_loc = jnp.einsum('btd,dhe->bhte', x_full, w_q, preferred_element_type=jnp.float32).astype(jnp.bfloat16)
        kv_loc = jnp.einsum('btd,nde->nbte', x_full, kv_weights, preferred_element_type=jnp.float32).astype(jnp.bfloat16)
        k_loc = kv_loc[0]
        v_loc = kv_loc[1]
        scores = jnp.einsum('bhqe,bke->bhqk', q_loc, k_loc, preferred_element_type=jnp.float32) * score_scale
        attn_prob = jax.nn.softmax(jnp.where(causal, scores, -jnp.inf), axis=-1)
        prob_bf = attn_prob.astype(jnp.bfloat16)
        out_loc = jnp.einsum('bhqk,bke->bhqe', prob_bf, v_loc, preferred_element_type=jnp.float32).astype(jnp.bfloat16)
        dout_loc = jnp.einsum('btd,hed->bhte', dy_full, w_o, preferred_element_type=jnp.float32).astype(jnp.bfloat16)
        grad_prob = jnp.einsum('bhqe,bke->bhqk', dout_loc, v_loc, preferred_element_type=jnp.float32)
        row_delta = jnp.einsum('bhqe,bhqe->bhq', dout_loc, out_loc, preferred_element_type=jnp.float32)
        grad_score = (attn_prob * (grad_prob - row_delta[..., None])).astype(jnp.bfloat16)
        grad_q = (jnp.einsum('bhqk,bke->bhqe', grad_score, k_loc, preferred_element_type=jnp.float32) * score_scale).astype(jnp.bfloat16)
        grad_k = jnp.einsum('bhqk,bhqe->bke', grad_score, q_loc, preferred_element_type=jnp.float32) * score_scale
        grad_v = jnp.einsum('bhqk,bhqe->bke', prob_bf, dout_loc, preferred_element_type=jnp.float32)
        grad_kv = jnp.stack([grad_k, grad_v]).astype(jnp.bfloat16)
        dx_part = (jnp.einsum('bhte,dhe->btd', grad_q, w_q, preferred_element_type=jnp.float32)
                   + jnp.einsum('nbte,nde->btd', grad_kv, kv_weights, preferred_element_type=jnp.float32))
        dwq_part = jnp.einsum('btd,bhte->dhe', x_full, grad_q, preferred_element_type=jnp.float32)
        dwkv_part = jnp.einsum('btd,nbte->nde', x_full, grad_kv, preferred_element_type=jnp.float32)
        dwo_part = jnp.einsum('bhte,btd->hed', out_loc, dy_full, preferred_element_type=jnp.float32)
        dx_loc = lax.psum_scatter(dx_part, 'model', scatter_dimension=1, tiled=True).astype(jnp.bfloat16)
        dwkv_sub = subgroup_scatter_sum(dwkv_part, sub_size, model_size)
        dwkv_loc = lax.psum_scatter(dwkv_sub, 'data', scatter_dimension=1, tiled=True)
        dwq_loc = lax.psum_scatter(dwq_part, 'data', scatter_dimension=0, tiled=True)
        dwo_loc = lax.psum_scatter(dwo_part, 'data', scatter_dimension=2, tiled=True)
        return dx_loc, dwq_loc, dwkv_loc[0], dwkv_loc[1], dwo_loc

    kv_rows = P(('pod', 'model', 'data'), None)
    return jax.shard_map(device_step, mesh=mesh,
                         in_specs=(tok_spec, tok_spec, P(None, 'model', None), P(), P(), P('model', None, None)),
                         out_specs=(tok_spec, P(('pod', 'data'), 'model', None), kv_rows, kv_rows, P(('pod', 'model'), None, 'data')),
                         check_vma=False)
```

profile of v0, /device:TPU:0, one launch (start us, length us, event | category | flops | bytes accessed | tf_op | source)
XLA Modules:
  0.0 1081.2 jit_solution(8604798977661764472)
XLA Ops:
  7.2 0.7 all-gather.5.cloned.1.call-update
  8.0 0.7 all-gather.3.cloned.1.call-update
  8.7 0.6 copy.35
  9.4 1.4 copy.34
  10.9 1.3 iota_compare_fusion
  12.1 16.8 %all-gather.5.cloned.1.call-done = bf16[1,1024,2048]{2,1,0:T(8,128)(2,1)} async-done(((bf16[1,512,2048]{2,1,0:T(8,128)(2,1)}), bf16[1,1024,2048]{2,1,0:T(8,128)(2,1)}) %all-gather.5.cloned.1.call-update) | async-done | bytes 4194320 | tf_op jit(solution)/shard_map/all_gather | solution.py:34
  28.9 10.7 bitcast_convert_fusion
  39.6 5.8 copy.65
  45.4 3.2 all-gather.3.cloned.1.call-done
  48.6 8.1 fusion.30
  56.8 2.4 fusion.41
  59.2 1.0 copy-done.12
  60.1 8.7 fusion.25
  68.8 19.3 %fusion.71 = (f32[4,1024]{1,0:T(4,128)S(1)}, f32[4,1024,1024]{1,2,0:T(8,128)}) fusion(f32[4,1024,1024]{1,2,0:T(8,128)} %fusion.25, pred[1024,1024]{0,1:T(8,128)(4,1)} %iota_compare_fusion), kind=kOutput, calls=%fused_computation.66 | output fusion | flops 25166848 | bytes 34619392 | tf_op jit(solution)/shard_map/sub | solution.py:44
  88.1 7.1 fusion.6
  95.2 2.4 fusion.60
  97.7 4.6 multiply_reduce_fusion
  102.3 10.1 multiply_convert_fusion
  112.4 5.9 fusion.63
  118.3 0.8 copy-done.10
  119.1 4.3 fusion.20
  123.5 6.6 reshape.132
  130.1 9.1 constant_dynamic-slice_fusion.2
  139.2 6.0 copy.53
  145.2 0.3 collective-permute-start
  145.5 4.0 copy.52
  149.5 4.0 bitcast_add_fusion.1
  153.5 0.3 all-reduce.3.cloned.1.call-start
  153.8 6.0 multiply_convert_fusion.1
  159.8 1.3 copy-done.18
  161.2 6.8 convolution_bitcast_fusion
  168.0 10.0 copy.50
  178.1 1.1 copy-done.7
  179.3 0.2 copy-done.11
  179.5 2.3 fusion.53
  181.8 0.5 copy-done.19
  182.4 7.0 fusion.2
  189.4 1.5 copy-done.17
  191.0 9.0 fusion.7
  200.0 0.6 copy-done.16
  200.6 0.6 dynamic-slice
  201.9 309.7 %reduce-scatter.6.cloned.1.call-done = f32[2,16,256]{2,1,0:T(8,128)} async-done(((f32[2,1024,256]{2,1,0:T(8,128)}), f32[2,16,256]{2,1,0:T(8,128)}) %reduce-scatter.6.cloned.1.call-update) | async-done | bytes 32784 | tf_op jit(solution)/shard_map/reduce_scatter | solution.py:62
  511.6 1.3 slice_bitcast_fusion.6
  512.9 167.7 %all-reduce.3.cloned.1.call-done = f32[2048,4,256]{2,1,0:T(4,128)} async-done(((f32[2048,4,256]{2,1,0:T(4,128)}), f32[2048,4,256]{2,1,0:T(4,128)}) %all-reduce.3.cloned.1.call-update) | async-done | bytes 8388624
  680.7 1.6 constant_dynamic-slice_fusion
  682.2 17.0 %reduce-scatter.4.cloned.1.call-done = f32[1,512,2048]{2,1,0:T(8,128)} async-done(((f32[1,1024,2048]{2,1,0:T(8,128)}), f32[1,512,2048]{2,1,0:T(8,128)}) %reduce-scatter.4.cloned.1.call-update) | async-done | bytes 4194320 | tf_op jit(solution)/shard_map/reduce_scatter | solution.py:60
  699.3 3.8 convert_element_type.64
  703.1 370.8 %reduce-scatter.8.cloned.1.call-done = f32[4,256,32]{1,2,0:T(8,128)} async-done(((f32[4,256,2048]{1,2,0:T(8,128)}), f32[4,256,32]{1,2,0:T(8,128)}) %reduce-scatter.8.cloned.1.call-update) | async-done | bytes 131088 | tf_op jit(solution)/shard_map/reduce_scatter | solution.py:64
  (44 shorter events, 0.5 us)
Async XLA Ops:
  7.2 1.6 copy-start.4
  7.2 2.2 copy-start.5
  7.2 21.7 %all-gather.5.cloned.1.call-start = ((), (), s32[]{:S(2)}) async-start(), calls=%async_computation.4 | async-start | bytes 6291456 | tf_op jit(solution)/shard_map/all_gather | solution.py:34
  7.9 40.7 %all-gather.3.cloned.1.call-start = ((), (), s32[]{:S(2)}) async-start(), calls=%async_computation.3 | async-start | bytes 6291456 | tf_op jit(solution)/shard_map/all_gather | solution.py:33
  8.7 502.9 %reduce-scatter.6.cloned.1.call-start = ((), (), s32[]{:S(2)}) async-start(), calls=%async_computation.6 | async-start | bytes 2129920 | tf_op jit(solution)/shard_map/reduce_scatter | solution.py:62
  48.6 8.2 copy-start
  48.6 8.2 copy-start.6
  59.2 1.0 copy-start.12
  88.1 7.1 copy-start.20
  95.2 2.4 copy-start.3
  95.2 2.5 copy-start.13
  97.7 20.6 %copy-start.8 = (bf16[1,1024,256]{2,1,0:T(8,128)(2,1)}, bf16[1,1024,256]{2,1,0:T(8,128)(2,1)S(1)}, u32[]{:S(2)}) copy-start(bf16[1,1024,256]{2,1,0:T(8,128)(2,1)S(1)} %fusion.60) | copy-start | bytes 1572868
  112.4 6.7 copy-start.1
  118.3 0.8 copy-start.10
  145.2 4.3 collective-permute-start
  149.5 4.3 copy-start.14
  153.5 527.2 %all-reduce.3.cloned.1.call-start = ((), (), s32[]{:S(2)}) async-start(), calls=%async_computation.8 | async-start | bytes 16777216
  153.8 7.4 copy-start.2
  159.8 1.3 copy-start.18
  178.0 1.2 copy-start.7
  178.0 1.4 copy-start.9
  178.0 1.5 copy-start.11
  178.0 521.3 %reduce-scatter.4.cloned.1.call-start = ((), (), s32[]{:S(2)}) async-start(), calls=%async_computation.5 | async-start | bytes 12582912 | tf_op jit(solution)/shard_map/reduce_scatter | solution.py:60
  179.5 2.3 copy-start.15
  179.5 2.9 copy-start.19
  189.4 1.6 copy-start.17
  189.4 884.5 %reduce-scatter.8.cloned.1.call-start = ((), (), s32[]{:S(2)}) async-start(), calls=%async_computation.7 | async-start | bytes 8519680 | tf_op jit(solution)/shard_map/reduce_scatter | solution.py:64
  200.0 0.7 copy-start.16
Sparse Core Ops, SparseCore 0:
  9.6 19.1 all-gather.4
  30.5 18.0 all-gather.2
  153.6 357.9 reduce-scatter.5
  516.8 163.8 all-reduce.2
  682.9 16.2 reduce-scatter.3
  702.1 371.7 reduce-scatter.7
where the time goes:
time: 1090 us; the launch traced here: 1080 us
  waiting for transfers between devices  887 us (81%)
  matrix products  88.4 us (8%)
  local copies, waits for them, and re-layouts  54.4 us (5%)
  other arithmetic  35.4 us (3%)
  between operations  15.5 us (1%)
    reduce_scatter x1, waiting for transfers between devices, device_step(): lax.psum_scatter(dwo_part, 'data', scatter_dimension=2, tiled=True)  371 us
    reduce_scatter x1, waiting for transfers between devices, device_step(): lax.psum_scatter(dwkv_sub, 'data', scatter_dimension=1, tiled=True)  310 us
    unnamed x7, waiting for transfers between devices  169 us
  transfers between devices with their start and end apart: 7, of which 6 were waited for; matrix products, arithmetic and copies ran while one was open for 7% of the time, Pallas kernels for 0%

commit v1 on v0

v1 whole, which is shorter than its diff:
```python
import jax
import jax.numpy as jnp
from jax import lax
from jax.experimental import pallas as pl
from jax.experimental.pallas import tpu as pltpu
from jax.sharding import PartitionSpec as P

MESH = pl.DeviceIdType.MESH
BF16 = jnp.bfloat16
F32 = jnp.float32
NS = 6
NG = 3
SIZES = (16, 4, 1)
SEQ, HALF, D, E, NH = 1024, 512, 2048, 256, 4
CD = E ** -0.5
LOG2E = 1.4426950408889634


def nn(a, b):
    return lax.dot_general(a, b, (((1,), (0,)), ((), ())), preferred_element_type=F32)


def nt(a, b):
    return lax.dot_general(a, b, (((1,), (1,)), ((), ())), preferred_element_type=F32)


def tn(a, b):
    return lax.dot_general(a, b, (((0,), (0,)), ((), ())), preferred_element_type=F32)


def loop(n, f):
    def body(i, _):
        f(i)
        return 0
    lax.fori_loop(0, n, body, 0)


def pick(i, a, b, c):
    return a * ((1 - i) * (2 - i) // 2) + b * (i * (2 - i)) + c * (i * (i - 1) // 2)


def slot(s, xc, yc, zc):
    k = s // 2
    return pick(k, xc * 16 + yc * 4 + zc, yc * 16 + zc * 4 + xc, zc * 16 + xc * 4 + yc)


class Ring:
    def __init__(self, bufs, recvs, send_sem, recv_sem):
        self.bufs, self.recvs, self.send_sem, self.recv_sem = bufs, recvs, send_sem, recv_sem
        d = lax.axis_index('data')
        self.d = d
        self.coord = (d % 4, (d // 4) % 4, d // 16)

    def greet(self, sem):
        for ax in range(3):
            for delta in (1, -1):
                c = self.coord[ax]
                to = self.d + ((c + delta + 4) % 4 - c) * 4 ** ax
                pl.semaphore_signal(sem, inc=1, device_id={'data': to}, device_id_type=MESH)

    def geom(self, s, p):
        ax = (s // 2 + p) % 3
        sg = 1 - 2 * (s % 2)
        c = pick(ax, *self.coord)
        stride = pick(ax, 1, 4, 16)
        return c, (c + 2) % 4, (c + sg + 4) % 4, (c - sg + 4) % 4, stride

    def msg(self, g, s, p, n):
        c, opp, fwd, back, stride = self.geom(s, p)
        part = (opp, back, fwd)[n]
        to = self.d + ((fwd, back, fwd)[n] - c) * stride
        size = SIZES[p]
        return pltpu.make_async_remote_copy(
            src_ref=self.bufs[p].at[g, s, pl.ds(part * size, size)], dst_ref=self.recvs[p].at[g, s, n],
            send_sem=self.send_sem.at[g, s, p, n], recv_sem=self.recv_sem.at[g, s, p, n],
            device_id={'data': to}, device_id_type=MESH)

    def start_one(self, g, s, p):
        self.msg(g, s, p, 0).start()
        self.msg(g, s, p, 1).start()

    def start(self, g):
        loop(NS, lambda s: self.start_one(g, s, 0))

    def middle(self, g, p):
        buf, rcv, size = self.bufs[p], self.recvs[p], SIZES[p]

        def one(s):
            fwd = self.geom(s, p)[2]
            self.msg(g, s, p, 0).wait_recv()

            def add(i):
                buf[g, s, fwd * size + i] = (buf[g, s, fwd * size + i].astype(F32) + rcv[g, s, 0, i].astype(F32)).astype(BF16)
            loop(size, add)
            self.msg(g, s, p, 2).start()
        loop(NS, one)

    def finish(self, g, p, out=None):
        buf, rcv, size = self.bufs[p], self.recvs[p], SIZES[p]

        def one(s):
            c = self.geom(s, p)[0]
            self.msg(g, s, p, 1).wait_recv()
            self.msg(g, s, p, 2).wait_recv()

            def total(i):
                v = buf[g, s, c * size + i].astype(F32) + rcv[g, s, 1, i].astype(F32) + rcv[g, s, 2, i].astype(F32)
                if p == 2:
                    out[g, s] = v
                else:
                    self.bufs[p + 1][g, s, i] = v.astype(BF16)
            loop(size, total)
            if p < 2:
                self.start_one(g, s, p + 1)
        loop(NS, one)

    def drain(self):
        def one(s):
            for g in range(NG):
                for p in range(3):
                    for n in range(3):
                        self.msg(g, s, p, n).wait_send()
        loop(NS, one)


def layer_kernel(x_hbm, dy_hbm, wq_hbm, wk_hbm, wv_hbm, wo_hbm, dx_hbm, out,
                 x, dy, wq, wkv, wo, q, do, kv, kvt, ot, dqt, dq, dkv, dkv_in, dkvb, dx_in,
                 b0, b1, b2, r0, r1, r2, load_sem, pair_send, pair_recv, send_sem, recv_sem):
    m = lax.axis_index('model')
    ring = Ring((b0, b1, b2), (r0, r1, r2), send_sem, recv_sem)
    own = pl.ds(pl.multiple_of(m * HALF, HALF), HALF)
    away = pl.ds(pl.multiple_of((1 - m) * HALF, HALF), HALF)

    def load(src, dst, i):
        return pltpu.make_async_copy(src, dst, load_sem.at[i])

    def push(src, dst, i):
        return pltpu.make_async_remote_copy(src_ref=src, dst_ref=dst, send_sem=pair_send.at[i], recv_sem=pair_recv.at[i],
                                            device_id={'model': 1 - m}, device_id_type=MESH)
    loads = [load(x_hbm, x.at[own], 0), load(wq_hbm, wq, 1), load(wk_hbm, wkv.at[:, 0:E], 2), load(wv_hbm, wkv.at[:, E:2 * E], 3),
             load(dy_hbm, dy.at[own], 4), load(wo_hbm, wo, 5)]
    for c in loads:
        c.start()
    sem = pltpu.get_barrier_semaphore()
    ring.greet(sem)
    pl.semaphore_signal(sem, inc=1, device_id={'model': 1 - m}, device_id_type=MESH)
    pl.semaphore_wait(sem, 7)
    push_x = push(x_hbm, x.at[own], 0)
    push_dy = push(dy_hbm, dy.at[own], 1)
    push_x.start()
    push_dy.start()
    dkv[...] = jnp.zeros_like(dkv)

    def project_x(rows):
        def head(h):
            cols = pl.ds(pl.multiple_of(h * E, E), E)
            q[h, rows] = nn(x[rows], wq[:, cols]).astype(BF16)
        loop(NH, head)

        def kv_part(i):
            cols = pl.ds(pl.multiple_of(i * E, E), E)
            kv[rows, cols] = nn(x[rows], wkv[:, cols]).astype(BF16)
        loop(2, kv_part)

    def project_dy(rows):
        def head(h):
            do[h, rows] = nt(dy[rows], wo[pl.ds(pl.multiple_of(h * E, E), E)]).astype(BF16)
        loop(NH, head)
    for c in loads[:4]:
        c.wait()
    project_x(own)
    loads[4].wait()
    loads[5].wait()
    project_dy(own)
    push_x.wait_recv()
    project_x(away)
    push_dy.wait_recv()
    project_dy(away)

    def turn(i):
        cols = pl.ds(pl.multiple_of(i * 256, 256), 256)
        kvt[0:E, cols] = kv[cols, 0:E].T
        kvt[E:2 * E, cols] = kv[cols, E:2 * E].T
    loop(4, turn)

    def attend(h, j):
        n = (j + 1) * 256
        rows = slice(j * 256, n)
        qb = q[h, rows]
        dob = do[h, rows]
        st = nt(kv[0:n, 0:E], qb)
        keep = lax.broadcasted_iota(jnp.int32, (256, 256), 0) <= lax.broadcasted_iota(jnp.int32, (256, 256), 1)
        diag = jnp.where(keep, st[n - 256:n], -jnp.inf)
        st = diag if j == 0 else jnp.concatenate([st[0:n - 256], diag], axis=0)
        top = jnp.max(st, axis=0, keepdims=True)
        pt = jnp.exp2((st - top) * (CD * LOG2E))
        pt = pt * (1.0 / jnp.sum(pt, axis=0, keepdims=True))
        pb = pt.astype(BF16)
        ob = nn(kvt[E:2 * E, 0:n], pb).astype(BF16)
        ot[:, rows] = ob
        delta = jnp.sum(dob.T.astype(F32) * ob.astype(F32), axis=0, keepdims=True)
        dpt = nt(kv[0:n, E:2 * E], dob)
        dst = (pt * (dpt - delta)).astype(BF16)
        dqb = (nn(kvt[0:E, 0:n], dst) * CD).astype(BF16)
        dqt[:, rows] = dqb
        dq[rows, pl.ds(pl.multiple_of(h * E, E), E)] = dqb.T
        dkv[0:n, 0:E] += nn(dst, qb)
        dkv[0:n, E:2 * E] += nn(pb, dob)

    def store_tiles(t, v, i):
        for u in range(2):
            tile = t + u
            g, s = tile // NS, tile % NS
            for j in range(8):
                at = slot(s, j % 4, (i % 2) * 2 + j // 4, i // 2)
                b0[g, s, at] = v[j * 32:(j + 1) * 32, u * 128:(u + 1) * 128]

    def weight_grad(lhs, rhs, t):
        def block(i):
            v = nn(lhs[...], rhs[:, pl.ds(pl.multiple_of(i * 256, 256), 256)]).astype(BF16).T
            store_tiles(t, v, i)
        loop(8, block)

    def at_head(h, hh, f):
        @pl.when(h == hh)
        def _():
            f()

    def head_step(h):
        attend(h, 0)
        at_head(h, 3, lambda: ring.finish(0, 1))
        attend(h, 1)
        at_head(h, 2, lambda: ring.middle(0, 0))
        at_head(h, 3, lambda: ring.middle(1, 0))
        attend(h, 2)
        at_head(h, 3, lambda: ring.middle(0, 2))
        attend(h, 3)
        weight_grad(ot, dy, h * 4)
        at_head(h, 1, lambda: ring.start(0))
        at_head(h, 2, lambda: ring.finish(0, 0))
        at_head(h, 3, lambda: ring.finish(0, 2, out))
        weight_grad(dqt, x, h * 4 + 2)
        at_head(h, 2, lambda: ring.start(1))
        at_head(h, 2, lambda: ring.middle(0, 1))
        at_head(h, 3, lambda: ring.finish(1, 0))
    loop(NH, head_step)

    push_kv = push(dkv, dkv_in, 2)
    push_kv.start()
    def dx_away(i):
        cols = pl.ds(pl.multiple_of(i * 256, 256), 256)
        wo[0:HALF, cols] = nt(dq[away], wq[cols]).astype(BF16)
    push_kv.wait_recv()

    def kv_sum(i):
        rows = pl.ds(pl.multiple_of(i * 128, 128), 128)
        v = dkv[rows] + dkv_in[rows]
        dkvb[rows, 0:E] = (v[:, 0:E] * CD).astype(BF16)
        dkvb[rows, E:2 * E] = v[:, E:2 * E].astype(BF16)
    loop(8, kv_sum)

    def kv_block(i):
        v = tn(x[:, pl.ds(pl.multiple_of(m * 1024 + i * 256, 256), 256)], dkvb[...]).astype(BF16)
        for j in range(16):
            rows = v[j * 16:(j + 1) * 16]
            for u in range(2):
                at = slot(4 + u, j % 4, j // 4, i)
                b0[2, 4 + u, at, 0:16] = rows[:, u * E:u * E + 128]
                b0[2, 4 + u, at, 16:32] = rows[:, u * E + 128:u * E + 256]
    loop(4, kv_block)
    ring.start(2)
    ring.middle(1, 1)
    loop(8, dx_away)
    push_dx = push(wo.at[pl.ds(0, HALF)], dx_in, 3)
    push_dx.start()
    ring.middle(2, 0)
    ring.finish(1, 1)

    def dx_own(i):
        cols = pl.ds(pl.multiple_of(i * 256, 256), 256)
        v = nt(dq[own], wq[cols]) + nt(dkvb[own], wkv[cols])
        wo[HALF:SEQ, cols] = (v + dx_in[:, cols].astype(F32)).astype(BF16)
    push_dx.wait_recv()
    loop(8, dx_own)
    store_dx = load(wo.at[pl.ds(HALF, HALF)], dx_hbm, 6)
    store_dx.start()
    ring.middle(1, 2)
    ring.finish(2, 0)
    ring.finish(1, 2, out)
    ring.middle(2, 1)
    ring.finish(2, 1)
    ring.middle(2, 2)
    ring.finish(2, 2, out)
    ring.drain()
    for c in (push_x, push_dy, push_kv, push_dx):
        c.wait_send()
    store_dx.wait()


def layer(x, dy, wq, wk, wv, wo):
    hbm = pl.BlockSpec(memory_space=pl.ANY)
    dma = pltpu.SemaphoreType.DMA
    bf = lambda *shape: pltpu.VMEM(shape, BF16)
    return pl.pallas_call(
        layer_kernel,
        out_shape=(jax.ShapeDtypeStruct((HALF, D), BF16), jax.ShapeDtypeStruct((NG, NS, 32, 128), F32)),
        in_specs=[hbm] * 6, out_specs=[hbm, pl.BlockSpec(memory_space=pltpu.VMEM)],
        scratch_shapes=[
            bf(SEQ, D), bf(SEQ, D), bf(D, NH * E), bf(D, 2 * E), bf(NH * E, D),
            bf(NH, SEQ, E), bf(NH, SEQ, E), bf(SEQ, 2 * E), bf(2 * E, SEQ), bf(E, SEQ), bf(E, SEQ), bf(SEQ, NH * E),
            pltpu.VMEM((SEQ, 2 * E), F32), pltpu.VMEM((SEQ, 2 * E), F32), bf(SEQ, 2 * E), bf(HALF, D),
            bf(NG, NS, 64, 32, 128), bf(NG, NS, 16, 32, 128), bf(NG, NS, 4, 32, 128),
            bf(NG, NS, 3, 16, 32, 128), bf(NG, NS, 3, 4, 32, 128), bf(NG, NS, 3, 1, 32, 128),
            dma((7,)), dma((4,)), dma((4,)), dma((NG, NS, 3, 3)), dma((NG, NS, 3, 3))],
        compiler_params=pltpu.CompilerParams(collective_id=0, has_side_effects=True, vmem_limit_bytes=67043328),
        cost_estimate=pl.CostEstimate(flops=3 * 10 ** 10, bytes_accessed=2 * 10 ** 7, transcendentals=0),
    )(x, dy, wq, wk, wv, wo)


def solution(mesh):
    tok_spec = P(('pod', 'data'), 'model', None)

    def device_step(x_loc, dy_loc, w_q, w_k, w_v, w_o):
        dx, out = layer(x_loc[0], dy_loc[0], w_q.reshape(D, NH * E), w_k[0], w_v[0], w_o.reshape(NH * E, D))
        tiles = out.reshape(NG * NS, 32, 128)
        heads = tiles[0:16].reshape(NH, 2, 2, 32, 128)
        dwo = heads[:, 0].transpose(0, 1, 3, 2).reshape(NH, E, 32)
        dwq = heads[:, 1].transpose(2, 0, 1, 3).reshape(32, NH, E)
        kv = tiles[16:18].reshape(2, 2, 16, 128).transpose(0, 2, 1, 3).reshape(2, 16, E)
        return dx[None], dwq, kv[0], kv[1], dwo

    kv_rows = P(('pod', 'model', 'data'), None)
    return jax.shard_map(device_step, mesh=mesh,
                         in_specs=(tok_spec, tok_spec, P(None, 'model', None), P(), P(), P('model', None, None)),
                         out_specs=(tok_spec, P(('pod', 'data'), 'model', None), kv_rows, kv_rows, P(('pod', 'model'), None, 'data')),
                         check_vma=False)
```

time: 1090 us -> 135 us (0.12)
  waiting for transfers between devices: 887 us -> 0 us
  Pallas kernels: 0 us -> 123 us
  matrix products: 88.4 us -> 0 us
  local copies, waits for them, and re-layouts: 54.4 us -> 10.8 us
  other arithmetic: 35.4 us -> 0 us
  between operations: 15.5 us -> 0.68 us
    reduce_scatter x3 -> x0, waiting for transfers between devices: 698 us -> none  [the longest x1 371 us: device_step(): lax.psum_scatter(dwo_part, 'data', scatter_dimension=2, tiled=True)]
    unnamed x7 -> x0, waiting for transfers between devices: 169 us -> none
    pallas_call x0 -> x1, Pallas kernels: none -> 123 us  [layer(): pl.pallas_call(layer_kernel, out_shape=(jax.ShapeDtypeStruct((HALF, D), B...]
    dot_general x14 -> x0, matrix products: 88.4 us -> none  [the longest x1 10.7 us: device_step(): jnp.einsum('btd,hed->bhte', dy_full, w_o, preferred_element_type=jnp.floa...]
    all_gather x2 -> x0, waiting for transfers between devices: 20 us -> none  [the longest x1 16.8 us: device_step(): dy_full = lax.all_gather(dy_loc, 'model', axis=1, tiled=True)]
    sub x1 -> x0, other arithmetic: 19.3 us -> none  [device_step(): attn_prob = jax.nn.softmax(jnp.where(causal, scores, -jnp.inf), axis=-1)]
    dynamic_slice x3 -> x0, local copies, waits for them, and re-layouts: 19.1 us -> none  [the longest x2 13.1 us: subgroup_scatter_sum(): lax.dynamic_index_in_dim(row_blocks, my_slot, axis=1, keepdims=False)]
    convert_element_type x2 -> x0, other arithmetic: 10.9 us -> none  [the longest x1 7.08 us: device_step(): prob_bf = attn_prob.astype(jnp.bfloat16)]
  transfers between devices with their start and end apart: 7 -> 0, of which waited for: 6 -> 0; matrix products, arithmetic and copies ran while one was open for 7% -> 0% of each run, Pallas kernels for 0% -> 0%
where the time goes in v1:
time: 135 us; the launch traced here: 134 us
  Pallas kernels  123 us (91%)
  local copies, waits for them, and re-layouts  10.8 us (8%)
    pallas_call x1, Pallas kernels, layer(): pl.pallas_call(layer_kernel, out_shape=(jax.ShapeDtypeStruct((HALF, D), B...  123 us
    unnamed x6, local copies, waits for them, and re-layouts  6.7 us

profile of v1, /device:TPU:0, one launch (start us, length us, event | category | flops | bytes accessed | tf_op | source)
XLA Modules:
  0.0 134.3 jit_solution(9011934066895675988)
XLA Ops:
  0.6 5.2 %copy.16 = bf16[256,8,4,256]{3,1,2,0:T(8,128)(2,1)} copy(bf16[256,8,4,256]{3,2,1,0:T(4,128)(2,1)} %bitcast.34) | data formatting | bytes 8388608
  5.8 122.9 %shard_map.101 = (bf16[512,2048]{1,0:T(8,128)(2,1)}, f32[3,6,32,128]{3,2,1,0:T(8,128)}) custom-call(bf16[512,2048]{1,0:T(8,128)(2,1)} %bitcast.47, bf16[512,2048]{1,0:T(8,128)(2,1)} %bitcast.48, bf16[2048,1024]{1,0:T(8,128)(2,1)} %bitcast.35, bf16[2048,256]{1,0:T(8,128)(2,1)} %bitcast.49, bf16[2048,256]{1,0:T(8,128)(2,1)} %bitcast.50, ...), custom_call_target="tpu_custom_call" | custom-call | flops 30000001024 | bytes 20000000 | tf_op jit(solution)/shard_map/pallas_call | solution.py:304
  128.7 0.0 copy-start
  128.7 0.9 slice.28
  129.6 1.0 slice.26
  130.6 0.6 copy_bitcast_fusion.3
  131.2 0.1 copy.24
  131.4 0.8 reshape.42
  132.1 0.1 copy.25
  132.2 0.8 reshape.40
  133.0 0.0 copy-done
  133.0 1.3 copy.28
  (3 shorter events, 0.0 us)
Async XLA Ops:
  128.7 4.3 %copy-start = (bf16[512,2048]{1,0:T(8,128)(2,1)S(1)}, bf16[512,2048]{1,0:T(8,128)(2,1)}, u32[]{:S(2)}) copy-start(bf16[512,2048]{1,0:T(8,128)(2,1)} %get-tuple-element.7) | copy-start | bytes 6291460

commit v2 on v1

v2 whole, which is shorter than its diff:
```python
import jax
import jax.numpy as jnp
from jax import lax
from jax.experimental import pallas as pl
from jax.experimental.pallas import tpu as pltpu
from jax.sharding import PartitionSpec as P

MESH = pl.DeviceIdType.MESH
BF16 = jnp.bfloat16
F32 = jnp.float32
NT = 18
SIZES = (16, 4, 1)
GROUPS = ((0, 4), (4, 8), (8, 12), (12, 16), (16, 18))
SEQ, HALF, D, E, NH = 1024, 512, 2048, 256, 4
CD = E ** -0.5
LOG2E = 1.4426950408889634


def nn(a, b):
    return lax.dot_general(a, b, (((1,), (0,)), ((), ())), preferred_element_type=F32)


def nt(a, b):
    return lax.dot_general(a, b, (((1,), (1,)), ((), ())), preferred_element_type=F32)


def tn(a, b):
    return lax.dot_general(a, b, (((0,), (0,)), ((), ())), preferred_element_type=F32)


def loop(n, f, start=0):
    def body(i, _):
        f(i)
        return 0
    lax.fori_loop(start, n, body, 0)


def block(i, size):
    return pl.ds(pl.multiple_of(i * size, size), size)


def pick(i, a, b, c):
    return a * ((1 - i) * (2 - i) // 2) + b * (i * (2 - i)) + c * (i * (i - 1) // 2)


def slot(t, xc, yc, zc):
    return pick((t // 2) % 3, xc * 16 + yc * 4 + zc, yc * 16 + zc * 4 + xc, zc * 16 + xc * 4 + yc)


class Ring:
    def __init__(self, bufs, recvs, send_sem, recv_sem, store):
        self.bufs, self.recvs, self.send_sem, self.recv_sem, self.store = bufs, recvs, send_sem, recv_sem, store
        d = lax.axis_index('data')
        self.d = d
        self.coord = (d % 4, (d // 4) % 4, d // 16)

    def greet(self, sem):
        for ax in range(3):
            for delta in (1, -1):
                c = self.coord[ax]
                to = self.d + ((c + delta + 4) % 4 - c) * 4 ** ax
                pl.semaphore_signal(sem, inc=1, device_id={'data': to}, device_id_type=MESH)

    def geom(self, t, p):
        ax = ((t // 2) % 3 + p) % 3
        sg = 1 - 2 * (t % 2)
        c = pick(ax, *self.coord)
        stride = pick(ax, 1, 4, 16)
        return c, (c + 2) % 4, (c + sg + 4) % 4, (c - sg + 4) % 4, stride

    def msg(self, t, p, n):
        c, opp, fwd, back, stride = self.geom(t, p)
        part = (opp, back, fwd)[n]
        to = self.d + ((fwd, back, fwd)[n] - c) * stride
        size = SIZES[p]
        return pltpu.make_async_remote_copy(
            src_ref=self.bufs[p].at[t, pl.ds(part * size, size)], dst_ref=self.recvs[p].at[t, n],
            send_sem=self.send_sem.at[t, p, n], recv_sem=self.recv_sem.at[t, p, n],
            device_id={'data': to}, device_id_type=MESH)

    def tiles(self, g, f):
        lo, hi = GROUPS[g]
        loop(hi, f, lo)

    def start_one(self, t, p):
        self.msg(t, p, 0).start()
        self.msg(t, p, 1).start()

    def start(self, g):
        self.tiles(g, lambda t: self.start_one(t, 0))

    def chunks(self, p, f):
        step = min(SIZES[p], 4)
        if SIZES[p] == step:
            f(0, step)
        else:
            loop(SIZES[p] // step, lambda i: f(i * step, step))

    def middle(self, g, p):
        buf, rcv, size = self.bufs[p], self.recvs[p], SIZES[p]

        def one(t):
            fwd = self.geom(t, p)[2]
            self.msg(t, p, 0).wait_recv()

            def add(i, w):
                at = pl.ds(fwd * size + i, w)
                buf[t, at] = (buf[t, at].astype(F32) + rcv[t, 0, pl.ds(i, w)].astype(F32)).astype(BF16)
            self.chunks(p, add)
            self.msg(t, p, 2).start()
        self.tiles(g, one)

    def finish(self, g, p):
        buf, rcv, size = self.bufs[p], self.recvs[p], SIZES[p]

        def total(t, i, w):
            c = self.geom(t, p)[0]
            return (buf[t, pl.ds(c * size + i, w)].astype(F32) + rcv[t, 1, pl.ds(i, w)].astype(F32)
                    + rcv[t, 2, pl.ds(i, w)].astype(F32))

        def one(t):
            self.msg(t, p, 1).wait_recv()
            self.msg(t, p, 2).wait_recv()
            if p == 2:
                self.store(t, total(t, 0, 1)[0])
                return

            def put(i, w):
                self.bufs[p + 1][t, pl.ds(i, w)] = total(t, i, w).astype(BF16)
            self.chunks(p, put)
            self.start_one(t, p + 1)
        if p == 2:
            for t in range(*GROUPS[g]):
                one(t)
        else:
            self.tiles(g, one)

    def drain(self):
        def one(t):
            for p in range(3):
                for n in range(3):
                    self.msg(t, p, n).wait_send()
        loop(NT, one)


def layer_kernel(x_hbm, dy_hbm, wq_hbm, wk_hbm, wv_hbm, wo_hbm, dx_hbm, dwq_out, dwk_out, dwv_out, dwo_out,
                 x, dy, wq, wkv, wo, q, do, kv, kvt, ot, dqt, dq, dkv, dkv_in, dkvb, dx_in,
                 b0, b1, b2, r0, r1, r2, load_sem, pair_send, pair_recv, send_sem, recv_sem):
    m = lax.axis_index('model')

    def store(t, v):
        if t >= 16:
            out = (dwk_out, dwv_out)[t - 16]
            out[:, 0:128] = v[0:16]
            out[:, 128:256] = v[16:32]
        else:
            h, u = divmod(t, 4)
            cols = slice((u % 2) * 128, (u % 2) * 128 + 128)
            if u < 2:
                dwo_out[h, :, cols] = v
            else:
                dwq_out[:, h, cols] = v
    ring = Ring((b0, b1, b2), (r0, r1, r2), send_sem, recv_sem, store)
    own = block(m, HALF)
    away = block(1 - m, HALF)

    def load(src, dst, i):
        return pltpu.make_async_copy(src, dst, load_sem.at[i])

    def push(src, dst, i):
        return pltpu.make_async_remote_copy(src_ref=src, dst_ref=dst, send_sem=pair_send.at[i], recv_sem=pair_recv.at[i],
                                            device_id={'model': 1 - m}, device_id_type=MESH)
    loads = [load(x_hbm, x.at[own], 0), load(wq_hbm, wq, 1), load(wk_hbm, wkv.at[:, 0:E], 2), load(wv_hbm, wkv.at[:, E:2 * E], 3),
             load(dy_hbm, dy.at[own], 4), load(wo_hbm, wo, 5)]
    for c in loads:
        c.start()
    sem = pltpu.get_barrier_semaphore()
    ring.greet(sem)
    pl.semaphore_signal(sem, inc=1, device_id={'model': 1 - m}, device_id_type=MESH)
    dkv[...] = jnp.zeros_like(dkv)
    pl.semaphore_wait(sem, 7)
    push_x = push(x_hbm, x.at[own], 0)
    push_dy = push(dy_hbm, dy.at[own], 1)
    push_x.start()
    push_dy.start()

    def project_x(rows):
        def pair(i):
            for h in range(2):
                q[i * 2 + h, rows] = nn(x[rows], wq[:, block(i * 2 + h, E)]).astype(BF16)
        loop(NH // 2, pair)
        kv[rows] = nn(x[rows], wkv[...]).astype(BF16)

    def project_dy(rows):
        def pair(i):
            for h in range(2):
                do[i * 2 + h, rows] = nt(dy[rows], wo[block(i * 2 + h, E)]).astype(BF16)
        loop(NH // 2, pair)
    for c in loads[:4]:
        c.wait()
    project_x(own)
    loads[4].wait()
    loads[5].wait()
    project_dy(own)
    push_x.wait_recv()
    project_x(away)
    push_dy.wait_recv()
    project_dy(away)

    def turn(i):
        cols = block(i, 256)
        kvt[0:E, cols] = kv[cols, 0:E].T
        kvt[E:2 * E, cols] = kv[cols, E:2 * E].T
    loop(4, turn)

    def attend(h, j):
        n = (j + 1) * 256
        rows = slice(j * 256, n)
        qb = q[h, rows]
        dob = do[h, rows]
        st = nt(kv[0:n, 0:E], qb)
        dpt = nt(kv[0:n, E:2 * E], dob)
        yield
        keep = lax.broadcasted_iota(jnp.int32, (256, 256), 0) <= lax.broadcasted_iota(jnp.int32, (256, 256), 1)
        diag = jnp.where(keep, st[n - 256:n], -jnp.inf)
        st = diag if j == 0 else jnp.concatenate([st[0:n - 256], diag], axis=0)
        top = jnp.max(st, axis=0, keepdims=True)
        pt = jnp.exp2((st - top) * (CD * LOG2E))
        pt = pt * (1.0 / jnp.sum(pt, axis=0, keepdims=True))
        pb = pt.astype(BF16)
        yield
        ob = nn(kvt[E:2 * E, 0:n], pb).astype(BF16)
        ot[:, rows] = ob
        delta = jnp.sum(dob.T.astype(F32) * ob.astype(F32), axis=0, keepdims=True)
        dkv[0:n, E:2 * E] += nn(pb, dob)
        yield
        dst = (pt * (dpt - delta)).astype(BF16)
        yield
        dqb = (nn(kvt[0:E, 0:n], dst) * CD).astype(BF16)
        dqt[:, rows] = dqb
        dq[rows, block(h, E)] = dqb.T
        dkv[0:n, 0:E] += nn(dst, qb)
        yield

    def attention(h):
        todo = [attend(h, j) for j in (3, 2, 1, 0)]
        for tick in range(5 + 2 * 3):
            for b, stages in enumerate(todo):
                if 0 <= tick - 2 * b < 5:
                    next(stages)

    def store_tiles(t, v, i):
        for u in range(2):
            for j in range(8):
                at = slot(t + u, j % 4, (i % 2) * 2 + j // 4, i // 2)
                b0[t + u, at] = v[j * 32:(j + 1) * 32, u * 128:(u + 1) * 128]

    def weight_grads(h):
        def step(i):
            vo = nn(ot[...], dy[:, block(i, 512)]).astype(BF16).T
            vq = nn(dqt[...], x[:, block(i, 512)]).astype(BF16).T
            for u in range(2):
                store_tiles(h * 4, vo[u * 256:(u + 1) * 256], i * 2 + u)
                store_tiles(h * 4 + 2, vq[u * 256:(u + 1) * 256], i * 2 + u)
        loop(4, step)
    push_kv = push(dkv, dkv_in, 2)

    def after_attention(h):
        if h == 1:
            ring.middle(0, 0)
        if h == 2:
            ring.finish(0, 0)
            ring.middle(1, 0)
        if h == 3:
            push_kv.start()
            ring.finish(0, 1)
            ring.finish(1, 0)
            ring.middle(2, 0)

    def after_grads(h):
        ring.start(h)
        if h == 2:
            ring.middle(0, 1)
        if h == 3:
            ring.middle(0, 2)
            ring.middle(1, 1)

    def head_step(h):
        attention(h)
        for hh in range(1, NH):
            @pl.when(h == hh)
            def _():
                after_attention(hh)
        weight_grads(h)
        for hh in range(NH):
            @pl.when(h == hh)
            def _():
                after_grads(hh)
    loop(NH, head_step)

    push_kv.wait_recv()

    def kv_sum(i):
        rows = block(i, 128)
        v = dkv[rows] + dkv_in[rows]
        dkvb[rows, 0:E] = (v[:, 0:E] * CD).astype(BF16)
        dkvb[rows, E:2 * E] = v[:, E:2 * E].astype(BF16)
    loop(8, kv_sum)

    def kv_block(i):
        v = tn(x[:, block(m * 4 + i, 256)], dkvb[...]).astype(BF16)
        for j in range(16):
            rows = v[j * 16:(j + 1) * 16]
            for u in range(2):
                at = slot(16 + u, j % 4, j // 4, i)
                b0[16 + u, at, 0:16] = rows[:, u * E:u * E + 128]
                b0[16 + u, at, 16:32] = rows[:, u * E + 128:u * E + 256]
    loop(4, kv_block)
    ring.start(4)
    ring.finish(2, 0)
    ring.finish(0, 2)
    ring.finish(1, 1)
    ring.middle(3, 0)

    def dx_away(i):
        cols = block(i, 512)
        wo[0:HALF, cols] = nt(dq[away], wq[cols]).astype(BF16)
    loop(4, dx_away)
    push_dx = push(wo.at[pl.ds(0, HALF)], dx_in, 3)
    push_dx.start()
    ring.middle(1, 2)
    ring.middle(2, 1)
    ring.middle(4, 0)

    def dx_own(i):
        cols = block(i, 512)
        v = nt(dq[own], wq[cols]) + nt(dkvb[own], wkv[cols])
        wo[HALF:SEQ, cols] = (v + dx_in[:, cols].astype(F32)).astype(BF16)
    push_dx.wait_recv()
    loop(2, dx_own)
    ring.finish(2, 1)
    ring.finish(3, 0)
    ring.finish(1, 2)
    loop(4, dx_own, 2)
    store_dx = load(wo.at[pl.ds(HALF, HALF)], dx_hbm, 6)
    store_dx.start()
    ring.middle(2, 2)
    ring.finish(4, 0)
    ring.middle(3, 1)
    ring.finish(2, 2)
    ring.finish(3, 1)
    ring.middle(4, 1)
    ring.middle(3, 2)
    ring.finish(4, 1)
    ring.finish(3, 2)
    ring.middle(4, 2)
    ring.finish(4, 2)
    ring.drain()
    for c in (push_x, push_dy, push_kv, push_dx):
        c.wait_send()
    store_dx.wait()


def layer(x, dy, wq, wk, wv, wo):
    hbm = pl.BlockSpec(memory_space=pl.ANY)
    dma = pltpu.SemaphoreType.DMA
    bf = lambda *shape: pltpu.VMEM(shape, BF16)
    return pl.pallas_call(
        layer_kernel,
        out_shape=(jax.ShapeDtypeStruct((HALF, D), BF16), jax.ShapeDtypeStruct((32, NH, E), F32),
                   jax.ShapeDtypeStruct((16, E), F32), jax.ShapeDtypeStruct((16, E), F32), jax.ShapeDtypeStruct((NH, 32, E), F32)),
        in_specs=[hbm] * 6, out_specs=[hbm] + [pl.BlockSpec(memory_space=pltpu.VMEM)] * 4,
        scratch_shapes=[
            bf(SEQ, D), bf(SEQ, D), bf(D, NH * E), bf(D, 2 * E), bf(NH * E, D),
            bf(NH, SEQ, E), bf(NH, SEQ, E), bf(SEQ, 2 * E), bf(2 * E, SEQ), bf(E, SEQ), bf(E, SEQ), bf(SEQ, NH * E),
            pltpu.VMEM((SEQ, 2 * E), F32), pltpu.VMEM((SEQ, 2 * E), F32), bf(SEQ, 2 * E), bf(HALF, D),
            bf(NT, 64, 32, 128), bf(NT, 16, 32, 128), bf(NT, 4, 32, 128),
            bf(NT, 3, 16, 32, 128), bf(NT, 3, 4, 32, 128), bf(NT, 3, 1, 32, 128),
            dma((7,)), dma((4,)), dma((4,)), dma((NT, 3, 3)), dma((NT, 3, 3))],
        compiler_params=pltpu.CompilerParams(collective_id=0, has_side_effects=True, vmem_limit_bytes=67043328),
        cost_estimate=pl.CostEstimate(flops=3 * 10 ** 10, bytes_accessed=2 * 10 ** 7, transcendentals=0),
    )(x, dy, wq, wk, wv, wo)


def solution(mesh):
    tok_spec = P(('pod', 'data'), 'model', None)

    def device_step(x_loc, dy_loc, w_q, w_k, w_v, w_o):
        dx, dwq, dwk, dwv, dwo = layer(x_loc[0], dy_loc[0], w_q.reshape(D, NH * E), w_k[0], w_v[0], w_o.reshape(NH * E, D))
        return dx[None], dwq, dwk, dwv, dwo.transpose(0, 2, 1)

    kv_rows = P(('pod', 'model', 'data'), None)
    return jax.shard_map(device_step, mesh=mesh,
                         in_specs=(tok_spec, tok_spec, P(None, 'model', None), P(), P(), P('model', None, None)),
                         out_specs=(tok_spec, P(('pod', 'data'), 'model', None), kv_rows, kv_rows, P(('pod', 'model'), None, 'data')),
                         check_vma=False)
```

time: 135 us -> 111 us (0.82)
  Pallas kernels: 123 us -> 98.9 us
    pallas_call x1, Pallas kernels: 123 us -> 98.9 us  [layer(): pl.pallas_call(layer_kernel, out_shape=(jax.ShapeDtypeStruct((HALF, D), B...]
    unnamed x6 -> x14, local copies, waits for them, and re-layouts: 6.7 us -> 10.9 us
    slice x4 -> x0, local copies, waits for them, and re-layouts: 1.9 us -> none  [the longest x1 0.97 us: device_step(): heads = tiles[0:16].reshape(NH, 2, 2, 32, 128)]
    reshape x3 -> x0, local copies, waits for them, and re-layouts: 1.56 us -> none  [the longest x1 0.78 us: device_step(): dwq = heads[:, 1].transpose(2, 0, 1, 3).reshape(32, NH, E)]
where the time goes in v2:
time: 111 us; the launch traced here: 110 us
  Pallas kernels  98.9 us (89%)
  local copies, waits for them, and re-layouts  10.9 us (10%)
    pallas_call x1, Pallas kernels, layer(): pl.pallas_call(layer_kernel, out_shape=(jax.ShapeDtypeStruct((HALF, D), B...  98.9 us
    unnamed x14, local copies, waits for them, and re-layouts  10.9 us

profile of v2, /device:TPU:0, one launch (start us, length us, event | category | flops | bytes accessed | tf_op | source)
XLA Modules:
  0.0 110.5 jit_solution(5373390653172384652)
XLA Ops:
  0.6 5.2 %copy.11 = bf16[256,8,4,256]{3,1,2,0:T(8,128)(2,1)} copy(bf16[256,8,4,256]{3,2,1,0:T(4,128)(2,1)} %bitcast.9) | data formatting | bytes 8388608
  5.8 98.9 %shard_map.101 = (bf16[512,2048]{1,0:T(8,128)(2,1)}, f32[32,4,256]{2,1,0:T(4,128)}, f32[16,256]{1,0:T(8,128)}, f32[16,256]{1,0:T(8,128)}, f32[4,32,256]{2,1,0:T(8,128)}) custom-call(bf16[512,2048]{1,0:T(8,128)(2,1)} %bitcast.14, bf16[512,2048]{1,0:T(8,128)(2,1)} %bitcast.15, bf16[2048,1024]{1,0:T(8,128)(2,1)} %bitcast.10, bf16[2048,256]{1,0:T(8,128)(2,1)} %bitcast.16, ...), custom_call_target="tpu_custom_call" | custom-call | flops 30000001024 | bytes 20000000 | tf_op jit(solution)/shard_map/pallas_call | solution.py:368
  104.7 0.0 copy-start.1
  104.7 0.0 copy-start.3
  104.7 0.0 copy-start.2
  104.7 0.0 copy-start
  104.7 3.2 %copy.17 = bf16[1,512,2048]{2,1,0:T(8,128)(2,1)} copy(bf16[1,512,2048]{2,1,0:T(8,128)(2,1)} %bitcast.11) | data formatting | bytes 4194304
  108.0 0.0 copy-done.1
  108.0 0.7 copy.18
  108.6 0.0 copy-done.3
  108.6 0.6 copy.19
  109.2 0.0 copy-done.2
  109.2 0.6 copy.20
  109.8 0.0 copy-done
  109.8 0.7 copy.21
Async XLA Ops:
  104.7 3.3 %copy-start.1 = (f32[32,4,256]{2,1,0:T(4,128)S(1)}, f32[32,4,256]{2,1,0:T(4,128)}, u32[]{:S(2)}) copy-start(f32[32,4,256]{2,1,0:T(4,128)} %get-tuple-element.21) | copy-start | bytes 393220
  104.7 3.9 %copy-start.3 = (f32[16,256]{1,0:T(8,128)S(1)}, f32[16,256]{1,0:T(8,128)}, u32[]{:S(2)}) copy-start(f32[16,256]{1,0:T(8,128)} %get-tuple-element.22) | copy-start | bytes 49156
  104.7 4.5 %copy-start.2 = (f32[16,256]{1,0:T(8,128)S(1)}, f32[16,256]{1,0:T(8,128)}, u32[]{:S(2)}) copy-start(f32[16,256]{1,0:T(8,128)} %get-tuple-element.23) | copy-start | bytes 49156
  104.7 5.1 %copy-start = (f32[4,32,256]{2,1,0:T(8,128)S(1)}, f32[4,32,256]{2,1,0:T(8,128)}, u32[]{:S(2)}) copy-start(f32[4,32,256]{2,1,0:T(8,128)} %get-tuple-element.14) | copy-start | bytes 393220

commit v3 on v2

--- a/solution.py
+++ b/solution.py
@@ -43,8 +43,9 @@
     return a * ((1 - i) * (2 - i) // 2) + b * (i * (2 - i)) + c * (i * (i - 1) // 2)
 
 
-def slot(t, xc, yc, zc):
-    return pick((t // 2) % 3, xc * 16 + yc * 4 + zc, yc * 16 + zc * 4 + xc, zc * 16 + xc * 4 + yc)
+def steps_of(t):
+    k = (t // 2) % 3
+    return pick(k, 16, 1, 4), pick(k, 4, 16, 1), pick(k, 1, 4, 16)
 
 
 class Ring:
@@ -56,7 +57,7 @@
 
     def greet(self, sem):
         for ax in range(3):
-            for delta in (1, -1):
+            for delta in (1, -1, 2):
                 c = self.coord[ax]
                 to = self.d + ((c + delta + 4) % 4 - c) * 4 ** ax
                 pl.semaphore_signal(sem, inc=1, device_id={'data': to}, device_id_type=MESH)
@@ -71,7 +72,8 @@
     def msg(self, t, p, n):
         c, opp, fwd, back, stride = self.geom(t, p)
         part = (opp, back, fwd)[n]
-        to = self.d + ((fwd, back, fwd)[n] - c) * stride
+        to = part if p == 2 else (fwd, back, fwd)[n]
+        to = self.d + (to - c) * stride
         size = SIZES[p]
         return pltpu.make_async_remote_copy(
             src_ref=self.bufs[p].at[t, pl.ds(part * size, size)], dst_ref=self.recvs[p].at[t, n],
@@ -82,12 +84,9 @@
         lo, hi = GROUPS[g]
         loop(hi, f, lo)
 
-    def start_one(self, t, p):
-        self.msg(t, p, 0).start()
-        self.msg(t, p, 1).start()
-
     def start(self, g):
-        self.tiles(g, lambda t: self.start_one(t, 0))
+        for n in range(2):
+            self.tiles(g, lambda t: self.msg(t, 0, n).start())
 
     def chunks(self, p, f):
         step = min(SIZES[p], 4)
@@ -115,12 +114,14 @@
 
         def total(t, i, w):
             c = self.geom(t, p)[0]
-            return (buf[t, pl.ds(c * size + i, w)].astype(F32) + rcv[t, 1, pl.ds(i, w)].astype(F32)
-                    + rcv[t, 2, pl.ds(i, w)].astype(F32))
+            v = buf[t, pl.ds(c * size + i, w)].astype(F32)
+            for n in range(0 if p == 2 else 1, 3):
+                v = v + rcv[t, n, pl.ds(i, w)].astype(F32)
+            return v
 
         def one(t):
-            self.msg(t, p, 1).wait_recv()
-            self.msg(t, p, 2).wait_recv()
+            for n in range(0 if p == 2 else 1, 3):
+                self.msg(t, p, n).wait_recv()
             if p == 2:
                 self.store(t, total(t, 0, 1)[0])
                 return
@@ -128,12 +129,14 @@
             def put(i, w):
                 self.bufs[p + 1][t, pl.ds(i, w)] = total(t, i, w).astype(BF16)
             self.chunks(p, put)
-            self.start_one(t, p + 1)
+            self.msg(t, p + 1, 0).start()
         if p == 2:
             for t in range(*GROUPS[g]):
                 one(t)
-        else:
-            self.tiles(g, one)
+            return
+        self.tiles(g, one)
+        for n in range(1, 3 if p == 1 else 2):
+            self.tiles(g, lambda t: self.msg(t, p + 1, n).start())
 
     def drain(self):
         def one(t):
@@ -178,34 +181,40 @@
     ring.greet(sem)
     pl.semaphore_signal(sem, inc=1, device_id={'model': 1 - m}, device_id_type=MESH)
     dkv[...] = jnp.zeros_like(dkv)
-    pl.semaphore_wait(sem, 7)
+    pl.semaphore_wait(sem, 10)
     push_x = push(x_hbm, x.at[own], 0)
     push_dy = push(dy_hbm, dy.at[own], 1)
     push_x.start()
     push_dy.start()
 
-    def project_x(rows):
-        def pair(i):
-            for h in range(2):
-                q[i * 2 + h, rows] = nn(x[rows], wq[:, block(i * 2 + h, E)]).astype(BF16)
-        loop(NH // 2, pair)
+    def project_q(h, rows):
+        q[h, rows] = nn(x[rows], wq[:, block(h, E)]).astype(BF16)
+
+    def project_do(h, rows):
+        do[h, rows] = nt(dy[rows], wo[block(h, E)]).astype(BF16)
+
+    def project_kv(rows):
         kv[rows] = nn(x[rows], wkv[...]).astype(BF16)
 
-    def project_dy(rows):
-        def pair(i):
-            for h in range(2):
-                do[i * 2 + h, rows] = nt(dy[rows], wo[block(i * 2 + h, E)]).astype(BF16)
-        loop(NH // 2, pair)
+    def project_x_own(i):
+        for h in range(2):
+            project_q(i * 2 + h, own)
+
+    def project_dy_own(i):
+        for h in range(2):
+            project_do(i * 2 + h, own)
     for c in loads[:4]:
         c.wait()
-    project_x(own)
+    loop(2, project_x_own)
+    project_kv(own)
     loads[4].wait()
     loads[5].wait()
-    project_dy(own)
+    loop(2, project_dy_own)
     push_x.wait_recv()
-    project_x(away)
+    project_kv(away)
+    project_q(0, away)
     push_dy.wait_recv()
-    project_dy(away)
+    project_do(0, away)
 
     def turn(i):
         cols = block(i, 256)
@@ -248,54 +257,65 @@
             for b, stages in enumerate(todo):
                 if 0 <= tick - 2 * b < 5:
                     next(stages)
+            if tick == 1:
+                project_q((h + 1) % NH, away)
+            if tick == 5:
+                project_do((h + 1) % NH, away)
 
     def store_tiles(t, v, i):
-        for u in range(2):
-            for j in range(8):
-                at = slot(t + u, j % 4, (i % 2) * 2 + j // 4, i // 2)
+        sx, sy, sz = steps_of(t)
+        base = (i % 2) * 2 * sy + (i // 2) * sz
+        for j in range(8):
+            at = base + (j % 4) * sx + (j // 4) * sy
+            for u in range(2):
                 b0[t + u, at] = v[j * 32:(j + 1) * 32, u * 128:(u + 1) * 128]
 
-    def weight_grads(h):
+    def weight_grads(h, half):
         def step(i):
             vo = nn(ot[...], dy[:, block(i, 512)]).astype(BF16).T
             vq = nn(dqt[...], x[:, block(i, 512)]).astype(BF16).T
             for u in range(2):
                 store_tiles(h * 4, vo[u * 256:(u + 1) * 256], i * 2 + u)
                 store_tiles(h * 4 + 2, vq[u * 256:(u + 1) * 256], i * 2 + u)
-        loop(4, step)
+        loop(half * 2 + 2, step, half * 2)
     push_kv = push(dkv, dkv_in, 2)
 
-    def after_attention(h):
-        if h == 1:
-            ring.middle(0, 0)
-        if h == 2:
-            ring.finish(0, 0)
-            ring.middle(1, 0)
-        if h == 3:
-            push_kv.start()
-            ring.finish(0, 1)
-            ring.finish(1, 0)
-            ring.middle(2, 0)
+    def amid_grads(h):
+        if h > 0:
+            ring.middle(h - 1, 0)
+        if h > 1:
+            ring.finish(h - 2, 0)
 
     def after_grads(h):
         ring.start(h)
-        if h == 2:
-            ring.middle(0, 1)
         if h == 3:
-            ring.middle(0, 2)
-            ring.middle(1, 1)
-
-    def head_step(h):
-        attention(h)
-        for hh in range(1, NH):
-            @pl.when(h == hh)
-            def _():
-                after_attention(hh)
-        weight_grads(h)
+            ring.finish(0, 1)
+
+    def at_head(h, f):
         for hh in range(NH):
             @pl.when(h == hh)
             def _():
-                after_grads(hh)
+                f(hh)
+
+    def head_step(h):
+        attention(h)
+
+        @pl.when(h == NH - 1)
+        def _():
+            push_kv.start()
+            ring.middle(0, 1)
+
+        def half_step(half):
+            weight_grads(h, half)
+
+            @pl.when(half == 0)
+            def _():
+                at_head(h, amid_grads)
+
+            @pl.when(half == 1)
+            def _():
+                at_head(h, after_grads)
+        loop(2, half_step)
     loop(NH, head_step)
 
     push_kv.wait_recv()
@@ -311,16 +331,13 @@
         v = tn(x[:, block(m * 4 + i, 256)], dkvb[...]).astype(BF16)
         for j in range(16):
             rows = v[j * 16:(j + 1) * 16]
+            at = i * 16 + (j % 4) * 4 + j // 4
             for u in range(2):
-                at = slot(16 + u, j % 4, j // 4, i)
                 b0[16 + u, at, 0:16] = rows[:, u * E:u * E + 128]
                 b0[16 + u, at, 16:32] = rows[:, u * E + 128:u * E + 256]
     loop(4, kv_block)
     ring.start(4)
-    ring.finish(2, 0)
-    ring.finish(0, 2)
-    ring.finish(1, 1)
-    ring.middle(3, 0)
+    ring.middle(1, 1)
 
     def dx_away(i):
         cols = block(i, 512)
@@ -328,9 +345,10 @@
     loop(4, dx_away)
     push_dx = push(wo.at[pl.ds(0, HALF)], dx_in, 3)
     push_dx.start()
-    ring.middle(1, 2)
-    ring.middle(2, 1)
-    ring.middle(4, 0)
+    ring.middle(3, 0)
+    ring.finish(0, 2)
+    ring.finish(1, 1)
+    ring.finish(2, 0)
 
     def dx_own(i):
         cols = block(i, 512)
@@ -338,22 +356,21 @@
         wo[HALF:SEQ, cols] = (v + dx_in[:, cols].astype(F32)).astype(BF16)
     push_dx.wait_recv()
     loop(2, dx_own)
-    ring.finish(2, 1)
-    ring.finish(3, 0)
-    ring.finish(1, 2)
+    ring.middle(4, 0)
+    ring.middle(2, 1)
     loop(4, dx_own, 2)
     store_dx = load(wo.at[pl.ds(HALF, HALF)], dx_hbm, 6)
     store_dx.start()
-    ring.middle(2, 2)
+    ring.finish(1, 2)
+    ring.finish(3, 0)
+    ring.finish(2, 1)
     ring.finish(4, 0)
     ring.middle(3, 1)
     ring.finish(2, 2)
+    ring.middle(4, 1)
     ring.finish(3, 1)
-    ring.middle(4, 1)
-    ring.middle(3, 2)
     ring.finish(4, 1)
     ring.finish(3, 2)
-    ring.middle(4, 2)
     ring.finish(4, 2)
     ring.drain()
     for c in (push_x, push_dy, push_kv, push_dx):

time: 111 us -> 99.1 us (0.89)
  Pallas kernels: 98.9 us -> 87.4 us
    pallas_call x1, Pallas kernels: 98.9 us -> 87.4 us  [layer(): pl.pallas_call(layer_kernel, out_shape=(jax.ShapeDtypeStruct((HALF, D), B...]
where the time goes in v3:
time: 99.1 us; the launch traced here: 99 us
  Pallas kernels  87.4 us (88%)
  local copies, waits for them, and re-layouts  10.9 us (11%)
    pallas_call x1, Pallas kernels, layer(): pl.pallas_call(layer_kernel, out_shape=(jax.ShapeDtypeStruct((HALF, D), B...  87.4 us
    unnamed x14, local copies, waits for them, and re-layouts  10.9 us

profile of v3, /device:TPU:0, one launch (start us, length us, event | category | flops | bytes accessed | tf_op | source)
XLA Modules:
  0.0 99.0 jit_solution(11653511802274391733)
XLA Ops:
  0.6 5.2 %copy.11 = bf16[256,8,4,256]{3,1,2,0:T(8,128)(2,1)} copy(bf16[256,8,4,256]{3,2,1,0:T(4,128)(2,1)} %bitcast.9) | data formatting | bytes 8388608
  5.8 87.4 %shard_map.101 = (bf16[512,2048]{1,0:T(8,128)(2,1)}, f32[32,4,256]{2,1,0:T(4,128)}, f32[16,256]{1,0:T(8,128)}, f32[16,256]{1,0:T(8,128)}, f32[4,32,256]{2,1,0:T(8,128)}) custom-call(bf16[512,2048]{1,0:T(8,128)(2,1)} %bitcast.14, bf16[512,2048]{1,0:T(8,128)(2,1)} %bitcast.15, bf16[2048,1024]{1,0:T(8,128)(2,1)} %bitcast.10, bf16[2048,256]{1,0:T(8,128)(2,1)} %bitcast.16, ...), custom_call_target="tpu_custom_call" | custom-call | flops 30000001024 | bytes 20000000 | tf_op jit(solution)/shard_map/pallas_call | solution.py:385
  93.2 0.0 copy-start.1
  93.2 0.0 copy-start.3
  93.2 0.0 copy-start.2
  93.2 0.0 copy-start
  93.2 3.2 %copy.17 = bf16[1,512,2048]{2,1,0:T(8,128)(2,1)} copy(bf16[1,512,2048]{2,1,0:T(8,128)(2,1)} %bitcast.11) | data formatting | bytes 4194304
  96.4 0.0 copy-done.1
  96.4 0.7 copy.18
  97.1 0.0 copy-done.3
  97.1 0.6 copy.19
  97.7 0.0 copy-done.2
  97.7 0.6 copy.20
  98.3 0.0 copy-done
  98.3 0.7 copy.21
Async XLA Ops:
  93.2 3.3 %copy-start.1 = (f32[32,4,256]{2,1,0:T(4,128)S(1)}, f32[32,4,256]{2,1,0:T(4,128)}, u32[]{:S(2)}) copy-start(f32[32,4,256]{2,1,0:T(4,128)} %get-tuple-element.21) | copy-start | bytes 393220
  93.2 3.9 %copy-start.3 = (f32[16,256]{1,0:T(8,128)S(1)}, f32[16,256]{1,0:T(8,128)}, u32[]{:S(2)}) copy-start(f32[16,256]{1,0:T(8,128)} %get-tuple-element.22) | copy-start | bytes 49156
  93.2 4.5 %copy-start.2 = (f32[16,256]{1,0:T(8,128)S(1)}, f32[16,256]{1,0:T(8,128)}, u32[]{:S(2)}) copy-start(f32[16,256]{1,0:T(8,128)} %get-tuple-element.23) | copy-start | bytes 49156
  93.2 5.1 %copy-start = (f32[4,32,256]{2,1,0:T(8,128)S(1)}, f32[4,32,256]{2,1,0:T(8,128)}, u32[]{:S(2)}) copy-start(f32[4,32,256]{2,1,0:T(8,128)} %get-tuple-element.14) | copy-start | bytes 393220

commit v4 on v3

--- a/solution.py
+++ b/solution.py
@@ -69,16 +69,25 @@
         stride = pick(ax, 1, 4, 16)
         return c, (c + 2) % 4, (c + sg + 4) % 4, (c - sg + 4) % 4, stride
 
-    def msg(self, t, p, n):
+    def direct(self, g, p):
+        return p == 2 or (p == 1 and g >= 3)
+
+    def msg(self, g, t, p, n):
         c, opp, fwd, back, stride = self.geom(t, p)
+        direct = self.direct(g, p)
         part = (opp, back, fwd)[n]
-        to = part if p == 2 else (fwd, back, fwd)[n]
+        to = part if direct else (fwd, back, fwd)[n]
         to = self.d + (to - c) * stride
         size = SIZES[p]
         return pltpu.make_async_remote_copy(
             src_ref=self.bufs[p].at[t, pl.ds(part * size, size)], dst_ref=self.recvs[p].at[t, n],
-            send_sem=self.send_sem.at[t, p, n], recv_sem=self.recv_sem.at[t, p, n],
+            send_sem=self.send_sem.at[g], recv_sem=self.recv_sem.at[g, p, 0 if n == 0 and not direct else 1],
             device_id={'data': to}, device_id_type=MESH)
+
+    def arrived(self, g, p, lo, hi):
+        first, last = GROUPS[g]
+        ref = self.recvs[p].at[pl.ds(first, last - first), pl.ds(lo, hi - lo)]
+        pltpu.make_async_copy(ref, ref, self.recv_sem.at[g, p, 0 if hi == 1 else 1]).wait()
 
     def tiles(self, g, f):
         lo, hi = GROUPS[g]
@@ -86,7 +95,7 @@
 
     def start(self, g):
         for n in range(2):
-            self.tiles(g, lambda t: self.msg(t, 0, n).start())
+            self.tiles(g, lambda t: self.msg(g, t, 0, n).start())
 
     def chunks(self, p, f):
         step = min(SIZES[p], 4)
@@ -100,28 +109,27 @@
 
         def one(t):
             fwd = self.geom(t, p)[2]
-            self.msg(t, p, 0).wait_recv()
 
             def add(i, w):
                 at = pl.ds(fwd * size + i, w)
                 buf[t, at] = (buf[t, at].astype(F32) + rcv[t, 0, pl.ds(i, w)].astype(F32)).astype(BF16)
             self.chunks(p, add)
-            self.msg(t, p, 2).start()
+            self.msg(g, t, p, 2).start()
+        self.arrived(g, p, 0, 1)
         self.tiles(g, one)
 
     def finish(self, g, p):
         buf, rcv, size = self.bufs[p], self.recvs[p], SIZES[p]
+        first = 0 if self.direct(g, p) else 1
 
         def total(t, i, w):
             c = self.geom(t, p)[0]
             v = buf[t, pl.ds(c * size + i, w)].astype(F32)
-            for n in range(0 if p == 2 else 1, 3):
+            for n in range(first, 3):
                 v = v + rcv[t, n, pl.ds(i, w)].astype(F32)
             return v
 
         def one(t):
-            for n in range(0 if p == 2 else 1, 3):
-                self.msg(t, p, n).wait_recv()
             if p == 2:
                 self.store(t, total(t, 0, 1)[0])
                 return
@@ -129,26 +137,25 @@
             def put(i, w):
                 self.bufs[p + 1][t, pl.ds(i, w)] = total(t, i, w).astype(BF16)
             self.chunks(p, put)
-            self.msg(t, p + 1, 0).start()
+            self.msg(g, t, p + 1, 0).start()
+        self.arrived(g, p, first, 3)
         if p == 2:
             for t in range(*GROUPS[g]):
                 one(t)
             return
         self.tiles(g, one)
-        for n in range(1, 3 if p == 1 else 2):
-            self.tiles(g, lambda t: self.msg(t, p + 1, n).start())
+        for n in range(1, 3 if self.direct(g, p + 1) else 2):
+            self.tiles(g, lambda t: self.msg(g, t, p + 1, n).start())
 
     def drain(self):
-        def one(t):
-            for p in range(3):
-                for n in range(3):
-                    self.msg(t, p, n).wait_send()
-        loop(NT, one)
-
-
-def layer_kernel(x_hbm, dy_hbm, wq_hbm, wk_hbm, wv_hbm, wo_hbm, dx_hbm, dwq_out, dwk_out, dwv_out, dwo_out,
-                 x, dy, wq, wkv, wo, q, do, kv, kvt, ot, dqt, dq, dkv, dkv_in, dkvb, dx_in,
-                 b0, b1, b2, r0, r1, r2, load_sem, pair_send, pair_recv, send_sem, recv_sem):
+        for g, (first, last) in enumerate(GROUPS):
+            ref = self.bufs[0].at[pl.ds(first, last - first), pl.ds(0, 63)]
+            pltpu.make_async_copy(ref, ref, self.send_sem.at[g]).wait()
+
+
+def layer_kernel(x_hbm, dy_hbm, wq_hbm, wk_hbm, wv_hbm, wo_hbm, dx_hbm, dwq_hbm, dwk_hbm, dwv_hbm, dwo_hbm,
+                 x, dy, wq_raw, wq, wkv, wo, q, do, kv, kvt, ot, dqt, dq, dkv, dkv_in, dkvb, dx_in,
+                 dwq_out, dwk_out, dwv_out, dwo_out, b0, b1, b2, r0, r1, r2, load_sem, pair_send, pair_recv, send_sem, recv_sem):
     m = lax.axis_index('model')
 
     def store(t, v):
@@ -173,14 +180,20 @@
     def push(src, dst, i):
         return pltpu.make_async_remote_copy(src_ref=src, dst_ref=dst, send_sem=pair_send.at[i], recv_sem=pair_recv.at[i],
                                             device_id={'model': 1 - m}, device_id_type=MESH)
-    loads = [load(x_hbm, x.at[own], 0), load(wq_hbm, wq, 1), load(wk_hbm, wkv.at[:, 0:E], 2), load(wv_hbm, wkv.at[:, E:2 * E], 3),
+    loads = [load(x_hbm, x.at[own], 0), load(wq_hbm, wq_raw, 1), load(wk_hbm, wkv.at[:, 0:E], 2), load(wv_hbm, wkv.at[:, E:2 * E], 3),
              load(dy_hbm, dy.at[own], 4), load(wo_hbm, wo, 5)]
-    for c in loads:
-        c.start()
+    for i in (1, 0, 2, 3, 4, 5):
+        loads[i].start()
     sem = pltpu.get_barrier_semaphore()
     ring.greet(sem)
     pl.semaphore_signal(sem, inc=1, device_id={'model': 1 - m}, device_id_type=MESH)
     dkv[...] = jnp.zeros_like(dkv)
+    loads[1].wait()
+
+    def flatten(i):
+        rows = block(i, 128)
+        wq[rows] = wq_raw[rows].reshape(128, NH * E)
+    loop(16, flatten)
     pl.semaphore_wait(sem, 10)
     push_x = push(x_hbm, x.at[own], 0)
     push_dy = push(dy_hbm, dy.at[own], 1)
@@ -196,20 +209,20 @@
     def project_kv(rows):
         kv[rows] = nn(x[rows], wkv[...]).astype(BF16)
 
-    def project_x_own(i):
+    def project_q_own(i):
         for h in range(2):
             project_q(i * 2 + h, own)
 
-    def project_dy_own(i):
+    def project_do_own(i):
         for h in range(2):
             project_do(i * 2 + h, own)
-    for c in loads[:4]:
-        c.wait()
-    loop(2, project_x_own)
+    for i in (0, 2, 3):
+        loads[i].wait()
+    loop(2, project_q_own)
     project_kv(own)
     loads[4].wait()
     loads[5].wait()
-    loop(2, project_dy_own)
+    loop(2, project_do_own)
     push_x.wait_recv()
     project_kv(away)
     project_q(0, away)
@@ -270,32 +283,13 @@
             for u in range(2):
                 b0[t + u, at] = v[j * 32:(j + 1) * 32, u * 128:(u + 1) * 128]
 
-    def weight_grads(h, half):
-        def step(i):
-            vo = nn(ot[...], dy[:, block(i, 512)]).astype(BF16).T
-            vq = nn(dqt[...], x[:, block(i, 512)]).astype(BF16).T
-            for u in range(2):
-                store_tiles(h * 4, vo[u * 256:(u + 1) * 256], i * 2 + u)
-                store_tiles(h * 4 + 2, vq[u * 256:(u + 1) * 256], i * 2 + u)
-        loop(half * 2 + 2, step, half * 2)
+    def weight_grads(h, i):
+        vo = nn(ot[...], dy[:, block(i, 512)]).astype(BF16).T
+        vq = nn(dqt[...], x[:, block(i, 512)]).astype(BF16).T
+        for u in range(2):
+            store_tiles(h * 4, vo[u * 256:(u + 1) * 256], i * 2 + u)
+            store_tiles(h * 4 + 2, vq[u * 256:(u + 1) * 256], i * 2 + u)
     push_kv = push(dkv, dkv_in, 2)
-
-    def amid_grads(h):
-        if h > 0:
-            ring.middle(h - 1, 0)
-        if h > 1:
-            ring.finish(h - 2, 0)
-
-    def after_grads(h):
-        ring.start(h)
-        if h == 3:
-            ring.finish(0, 1)
-
-    def at_head(h, f):
-        for hh in range(NH):
-            @pl.when(h == hh)
-            def _():
-                f(hh)
 
     def head_step(h):
         attention(h)
@@ -305,18 +299,23 @@
             push_kv.start()
             ring.middle(0, 1)
 
-        def half_step(half):
-            weight_grads(h, half)
-
-            @pl.when(half == 0)
-            def _():
-                at_head(h, amid_grads)
-
-            @pl.when(half == 1)
-            def _():
-                at_head(h, after_grads)
-        loop(2, half_step)
+        def grads_step(i):
+            weight_grads(h, i)
+
+            def at(hh, ii, f):
+                @pl.when((h == hh) & (i == ii))
+                def _():
+                    f()
+            for hh in range(2, NH):
+                at(hh, 0, lambda: ring.finish(hh - 2, 0))
+            for hh in range(1, NH):
+                at(hh, 2, lambda: ring.middle(hh - 1, 0))
+            for hh in range(NH):
+                at(hh, 3, lambda: ring.start(hh))
+        loop(4, grads_step)
     loop(NH, head_step)
+    ring.finish(0, 1)
+    ring.middle(1, 1)
 
     push_kv.wait_recv()
 
@@ -337,43 +336,52 @@
                 b0[16 + u, at, 16:32] = rows[:, u * E + 128:u * E + 256]
     loop(4, kv_block)
     ring.start(4)
-    ring.middle(1, 1)
 
     def dx_away(i):
         cols = block(i, 512)
         wo[0:HALF, cols] = nt(dq[away], wq[cols]).astype(BF16)
-    loop(4, dx_away)
-    push_dx = push(wo.at[pl.ds(0, HALF)], dx_in, 3)
-    push_dx.start()
+    def push_dx(i):
+        cols = pl.ds(i * 1024, 1024)
+        return push(wo.at[pl.ds(0, HALF), cols], dx_in.at[:, cols], 3 + i)
+    loop(2, dx_away)
+    push_dx(0).start()
     ring.middle(3, 0)
+    ring.finish(2, 0)
+    loop(4, dx_away, 2)
+    push_dx(1).start()
+    ring.middle(4, 0)
+    ring.finish(1, 1)
     ring.finish(0, 2)
-    ring.finish(1, 1)
-    ring.finish(2, 0)
 
     def dx_own(i):
         cols = block(i, 512)
         v = nt(dq[own], wq[cols]) + nt(dkvb[own], wkv[cols])
         wo[HALF:SEQ, cols] = (v + dx_in[:, cols].astype(F32)).astype(BF16)
-    push_dx.wait_recv()
-    loop(2, dx_own)
-    ring.middle(4, 0)
+    push_dx(0).wait_recv()
+    loop(1, dx_own)
     ring.middle(2, 1)
-    loop(4, dx_own, 2)
+    ring.finish(3, 0)
+    loop(2, dx_own, 1)
+    ring.finish(4, 0)
+    push_dx(1).wait_recv()
+    loop(3, dx_own, 2)
+    ring.finish(2, 1)
+    ring.finish(1, 2)
+    loop(4, dx_own, 3)
     store_dx = load(wo.at[pl.ds(HALF, HALF)], dx_hbm, 6)
     store_dx.start()
-    ring.finish(1, 2)
-    ring.finish(3, 0)
-    ring.finish(2, 1)
-    ring.finish(4, 0)
-    ring.middle(3, 1)
-    ring.finish(2, 2)
-    ring.middle(4, 1)
     ring.finish(3, 1)
     ring.finish(4, 1)
-    ring.finish(3, 2)
-    ring.finish(4, 2)
+    for g in (2, 3, 4):
+        ring.finish(g, 2)
+    stores = [load(a, b, 7 + i) for i, (a, b) in enumerate(
+        ((dwq_out, dwq_hbm), (dwk_out, dwk_hbm), (dwv_out, dwv_hbm), (dwo_out, dwo_hbm)))]
+    for c in stores:
+        c.start()
     ring.drain()
-    for c in (push_x, push_dy, push_kv, push_dx):
+    for c in stores:
+        c.wait()
+    for c in (push_x, push_dy, push_kv, push_dx(0), push_dx(1)):
         c.wait_send()
     store_dx.wait()
 
@@ -386,24 +394,50 @@
         layer_kernel,
         out_shape=(jax.ShapeDtypeStruct((HALF, D), BF16), jax.ShapeDtypeStruct((32, NH, E), F32),
                    jax.ShapeDtypeStruct((16, E), F32), jax.ShapeDtypeStruct((16, E), F32), jax.ShapeDtypeStruct((NH, 32, E), F32)),
-        in_specs=[hbm] * 6, out_specs=[hbm] + [pl.BlockSpec(memory_space=pltpu.VMEM)] * 4,
+        in_specs=[hbm] * 6, out_specs=[hbm] * 5,
         scratch_shapes=[
-            bf(SEQ, D), bf(SEQ, D), bf(D, NH * E), bf(D, 2 * E), bf(NH * E, D),
+            bf(SEQ, D), bf(SEQ, D), bf(D, NH, E), bf(D, NH * E), bf(D, 2 * E), bf(NH * E, D),
             bf(NH, SEQ, E), bf(NH, SEQ, E), bf(SEQ, 2 * E), bf(2 * E, SEQ), bf(E, SEQ), bf(E, SEQ), bf(SEQ, NH * E),
             pltpu.VMEM((SEQ, 2 * E), F32), pltpu.VMEM((SEQ, 2 * E), F32), bf(SEQ, 2 * E), bf(HALF, D),
+            pltpu.VMEM((32, NH, E), F32), pltpu.VMEM((16, E), F32), pltpu.VMEM((16, E), F32), pltpu.VMEM((NH, 32, E), F32),
             bf(NT, 64, 32, 128), bf(NT, 16, 32, 128), bf(NT, 4, 32, 128),
             bf(NT, 3, 16, 32, 128), bf(NT, 3, 4, 32, 128), bf(NT, 3, 1, 32, 128),
-            dma((7,)), dma((4,)), dma((4,)), dma((NT, 3, 3)), dma((NT, 3, 3))],
+            dma((11,)), dma((5,)), dma((5,)), dma((len(GROUPS),)), dma((len(GROUPS), 3, 2))],
         compiler_params=pltpu.CompilerParams(collective_id=0, has_side_effects=True, vmem_limit_bytes=67043328),
         cost_estimate=pl.CostEstimate(flops=3 * 10 ** 10, bytes_accessed=2 * 10 ** 7, transcendentals=0),
     )(x, dy, wq, wk, wv, wo)
 
 
+def hand_on_kernel(dx, dwq, dwk, dwv, dwo, dx_out, dwq_out, dwk_out, dwv_out, dwo_out, dx_v, dwq_v, dwk_v, dwv_v, dwo_v, sem_in, sem_out):
+    pieces = [(dx.at[pl.ds(i * 128, 128)], dx_v.at[pl.ds(i * 128, 128)], dx_out.at[pl.ds(i * 128, 128)]) for i in range(4)]
+    pieces += [(dwq, dwq_v, dwq_out), (dwk, dwk_v, dwk_out), (dwv, dwv_v, dwv_out), (dwo, dwo_v, dwo_out)]
+    reads = [pltpu.make_async_copy(a, b, sem_in.at[i]) for i, (a, b, _) in enumerate(pieces)]
+    writes = [pltpu.make_async_copy(b, c, sem_out.at[i]) for i, (_, b, c) in enumerate(pieces)]
+    for c in reads:
+        c.start()
+    for r, w in zip(reads, writes):
+        r.wait()
+        w.start()
+    for w in writes:
+        w.wait()
+
+
+def hand_on(*arrays):
+    hbm = pl.BlockSpec(memory_space=pl.ANY)
+    return pl.pallas_call(
+        hand_on_kernel,
+        out_shape=tuple(jax.ShapeDtypeStruct(a.shape, a.dtype) for a in arrays),
+        in_specs=[hbm] * 5, out_specs=[hbm] * 5,
+        scratch_shapes=[pltpu.VMEM(a.shape, a.dtype) for a in arrays] + [pltpu.SemaphoreType.DMA((8,)), pltpu.SemaphoreType.DMA((8,))],
+        cost_estimate=pl.CostEstimate(flops=10 ** 6, bytes_accessed=6 * 10 ** 6, transcendentals=0),
+    )(*arrays)
+
+
 def solution(mesh):
     tok_spec = P(('pod', 'data'), 'model', None)
 
     def device_step(x_loc, dy_loc, w_q, w_k, w_v, w_o):
-        dx, dwq, dwk, dwv, dwo = layer(x_loc[0], dy_loc[0], w_q.reshape(D, NH * E), w_k[0], w_v[0], w_o.reshape(NH * E, D))
+        dx, dwq, dwk, dwv, dwo = hand_on(*layer(x_loc[0], dy_loc[0], w_q, w_k[0], w_v[0], w_o.reshape(NH * E, D)))
         return dx[None], dwq, dwk, dwv, dwo.transpose(0, 2, 1)
 
     kv_rows = P(('pod', 'model', 'data'), None)

time: 99.1 us -> 85.3 us (0.86)
  local copies, waits for them, and re-layouts: 10.9 us -> 0 us
  Pallas kernels: 87.4 us -> 84.3 us
    unnamed x14 -> x0, local copies, waits for them, and re-layouts: 10.9 us -> none
    pallas_call x1, Pallas kernels: 87.4 us -> 81.7 us  [layer(): pl.pallas_call(layer_kernel, out_shape=(jax.ShapeDtypeStruct((HALF, D), B...]
    pallas_call x0 -> x1, Pallas kernels: none -> 2.58 us  [hand_on(): pl.pallas_call(hand_on_kernel, out_shape=tuple((jax.ShapeDtypeStruct(a.sh...]
where the time goes in v4:
time: 85.3 us; the launch traced here: 85.1 us
  Pallas kernels  84.3 us (99%)
    pallas_call x1, Pallas kernels, layer(): pl.pallas_call(layer_kernel, out_shape=(jax.ShapeDtypeStruct((HALF, D), B...  81.7 us
    pallas_call x1, Pallas kernels, hand_on(): pl.pallas_call(hand_on_kernel, out_shape=tuple((jax.ShapeDtypeStruct(a.sh...  2.58 us

profile of v4, /device:TPU:0, one launch (start us, length us, event | category | flops | bytes accessed | tf_op | source)
XLA Modules:
  0.0 85.1 jit_solution(12148318707635424087)
XLA Ops:
  0.6 81.7 %shard_map.101 = (bf16[512,2048]{1,0:T(8,128)(2,1)}, f32[32,4,256]{2,1,0:T(4,128)}, f32[16,256]{1,0:T(8,128)}, f32[16,256]{1,0:T(8,128)}, f32[4,32,256]{2,1,0:T(8,128)}) custom-call(bf16[512,2048]{1,0:T(8,128)(2,1)} %bitcast.8, bf16[512,2048]{1,0:T(8,128)(2,1)} %bitcast.9, bf16[2048,4,256]{2,1,0:T(4,128)(2,1)} %wq_hbm.1, bf16[2048,256]{1,0:T(8,128)(2,1)} %bitcast.11, ...), custom_call_target="tpu_custom_call" | custom-call | flops 30000001024 | bytes 20000000 | tf_op jit(solution)/shard_map/pallas_call | solution.py:393
  82.4 2.6 %shard_map.102 = (bf16[512,2048]{1,0:T(8,128)(2,1)}, f32[32,4,256]{2,1,0:T(4,128)}, f32[16,256]{1,0:T(8,128)}, f32[16,256]{1,0:T(8,128)}, f32[4,32,256]{2,1,0:T(8,128)}) custom-call(bf16[512,2048]{1,0:T(8,128)(2,1)} %get-tuple-element.15.dx, f32[32,4,256]{2,1,0:T(4,128)} %get-tuple-element.16.dwq, f32[16,256]{1,0:T(8,128)} %get-tuple-element.17.dwk, ...), custom_call_target="tpu_custom_call" | custom-call | flops 1000000 | bytes 6000000 | tf_op jit(solution)/shard_map/pallas_call | solution.py:427

commit v5 on v4

--- a/solution.py
+++ b/solution.py
@@ -52,37 +52,31 @@
     def __init__(self, bufs, recvs, send_sem, recv_sem, store):
         self.bufs, self.recvs, self.send_sem, self.recv_sem, self.store = bufs, recvs, send_sem, recv_sem, store
         d = lax.axis_index('data')
-        self.d = d
-        self.coord = (d % 4, (d // 4) % 4, d // 16)
+        coords = (d % 4, (d // 4) % 4, d // 16)
+        self.at = [[((c + k) % 4, d + ((c + k) % 4 - c) * 4 ** ax) for k in range(4)] for ax, c in enumerate(coords)]
 
     def greet(self, sem):
         for ax in range(3):
-            for delta in (1, -1, 2):
-                c = self.coord[ax]
-                to = self.d + ((c + delta + 4) % 4 - c) * 4 ** ax
-                pl.semaphore_signal(sem, inc=1, device_id={'data': to}, device_id_type=MESH)
-
-    def geom(self, t, p):
-        ax = ((t // 2) % 3 + p) % 3
-        sg = 1 - 2 * (t % 2)
-        c = pick(ax, *self.coord)
-        stride = pick(ax, 1, 4, 16)
-        return c, (c + 2) % 4, (c + sg + 4) % 4, (c - sg + 4) % 4, stride
+            for k in (1, 3, 2):
+                pl.semaphore_signal(sem, inc=1, device_id={'data': self.at[ax][k][1]}, device_id_type=MESH)
+
+    def ways(self, t, p):
+        ring = self.at[((t // 2) % 3 + p) % 3]
+        return (ring[0], ring[2], ring[1], ring[3]) if t % 2 == 0 else (ring[0], ring[2], ring[3], ring[1])
 
     def direct(self, g, p):
         return p == 2 or (p == 1 and g >= 3)
 
     def msg(self, g, t, p, n):
-        c, opp, fwd, back, stride = self.geom(t, p)
+        _, opp, fwd, back = self.ways(t, p)
         direct = self.direct(g, p)
         part = (opp, back, fwd)[n]
         to = part if direct else (fwd, back, fwd)[n]
-        to = self.d + (to - c) * stride
         size = SIZES[p]
         return pltpu.make_async_remote_copy(
-            src_ref=self.bufs[p].at[t, pl.ds(part * size, size)], dst_ref=self.recvs[p].at[t, n],
+            src_ref=self.bufs[p].at[t, pl.ds(part[0] * size, size)], dst_ref=self.recvs[p].at[t, n],
             send_sem=self.send_sem.at[g], recv_sem=self.recv_sem.at[g, p, 0 if n == 0 and not direct else 1],
-            device_id={'data': to}, device_id_type=MESH)
+            device_id={'data': to[1]}, device_id_type=MESH)
 
     def arrived(self, g, p, lo, hi):
         first, last = GROUPS[g]
@@ -90,25 +84,23 @@
         pltpu.make_async_copy(ref, ref, self.recv_sem.at[g, p, 0 if hi == 1 else 1]).wait()
 
     def tiles(self, g, f):
-        lo, hi = GROUPS[g]
-        loop(hi, f, lo)
+        for t in range(*GROUPS[g]):
+            f(t)
 
     def start(self, g):
         for n in range(2):
             self.tiles(g, lambda t: self.msg(g, t, 0, n).start())
 
     def chunks(self, p, f):
-        step = min(SIZES[p], 4)
-        if SIZES[p] == step:
-            f(0, step)
-        else:
-            loop(SIZES[p] // step, lambda i: f(i * step, step))
+        step = min(SIZES[p], 8)
+        for i in range(0, SIZES[p], step):
+            f(i, step)
 
     def middle(self, g, p):
         buf, rcv, size = self.bufs[p], self.recvs[p], SIZES[p]
 
         def one(t):
-            fwd = self.geom(t, p)[2]
+            fwd = self.ways(t, p)[2][0]
 
             def add(i, w):
                 at = pl.ds(fwd * size + i, w)
@@ -123,7 +115,7 @@
         first = 0 if self.direct(g, p) else 1
 
         def total(t, i, w):
-            c = self.geom(t, p)[0]
+            c = self.ways(t, p)[0][0]
             v = buf[t, pl.ds(c * size + i, w)].astype(F32)
             for n in range(first, 3):
                 v = v + rcv[t, n, pl.ds(i, w)].astype(F32)
@@ -139,13 +131,10 @@
             self.chunks(p, put)
             self.msg(g, t, p + 1, 0).start()
         self.arrived(g, p, first, 3)
-        if p == 2:
-            for t in range(*GROUPS[g]):
-                one(t)
-            return
         self.tiles(g, one)
-        for n in range(1, 3 if self.direct(g, p + 1) else 2):
-            self.tiles(g, lambda t: self.msg(g, t, p + 1, n).start())
+        if p < 2:
+            for n in range(1, 3 if self.direct(g, p + 1) else 2):
+                self.tiles(g, lambda t: self.msg(g, t, p + 1, n).start())
 
     def drain(self):
         for g, (first, last) in enumerate(GROUPS):
@@ -182,58 +171,57 @@
                                             device_id={'model': 1 - m}, device_id_type=MESH)
     loads = [load(x_hbm, x.at[own], 0), load(wq_hbm, wq_raw, 1), load(wk_hbm, wkv.at[:, 0:E], 2), load(wv_hbm, wkv.at[:, E:2 * E], 3),
              load(dy_hbm, dy.at[own], 4), load(wo_hbm, wo, 5)]
-    for i in (1, 0, 2, 3, 4, 5):
+    for i in (0, 2, 3, 1, 4, 5):
         loads[i].start()
     sem = pltpu.get_barrier_semaphore()
     ring.greet(sem)
     pl.semaphore_signal(sem, inc=1, device_id={'model': 1 - m}, device_id_type=MESH)
     dkv[...] = jnp.zeros_like(dkv)
-    loads[1].wait()
+
+    def project_q(h, rows):
+        q[h, rows] = nn(x[rows], wq[:, block(h, E)]).astype(BF16)
+
+    def project_do(h, rows):
+        do[h, rows] = nt(dy[rows], wo[block(h, E)]).astype(BF16)
+
+    def project_q_own(i):
+        for h in range(2):
+            project_q(i * 2 + h, own)
+
+    def project_do_own(i):
+        for h in range(2):
+            project_do(i * 2 + h, own)
 
     def flatten(i):
         rows = block(i, 128)
         wq[rows] = wq_raw[rows].reshape(128, NH * E)
-    loop(16, flatten)
-    pl.semaphore_wait(sem, 10)
-    push_x = push(x_hbm, x.at[own], 0)
-    push_dy = push(dy_hbm, dy.at[own], 1)
-    push_x.start()
-    push_dy.start()
-
-    def project_q(h, rows):
-        q[h, rows] = nn(x[rows], wq[:, block(h, E)]).astype(BF16)
-
-    def project_do(h, rows):
-        do[h, rows] = nt(dy[rows], wo[block(h, E)]).astype(BF16)
-
-    def project_kv(rows):
-        kv[rows] = nn(x[rows], wkv[...]).astype(BF16)
-
-    def project_q_own(i):
-        for h in range(2):
-            project_q(i * 2 + h, own)
-
-    def project_do_own(i):
-        for h in range(2):
-            project_do(i * 2 + h, own)
-    for i in (0, 2, 3):
-        loads[i].wait()
-    loop(2, project_q_own)
-    project_kv(own)
-    loads[4].wait()
-    loads[5].wait()
-    loop(2, project_do_own)
-    push_x.wait_recv()
-    project_kv(away)
-    project_q(0, away)
-    push_dy.wait_recv()
-    project_do(0, away)
 
     def turn(i):
         cols = block(i, 256)
         kvt[0:E, cols] = kv[cols, 0:E].T
         kvt[E:2 * E, cols] = kv[cols, E:2 * E].T
+    for i in (0, 2, 3):
+        loads[i].wait()
+    kv[own] = nn(x[own], wkv[...]).astype(BF16)
+    pl.semaphore_wait(sem, 10)
+    push_k = push(kv.at[own], kv.at[own], 5)
+    push_x = push(x_hbm, x.at[own], 0)
+    push_dy = push(dy_hbm, dy.at[own], 1)
+    push_k.start()
+    push_x.start()
+    push_dy.start()
+    loads[1].wait()
+    loop(16, flatten)
+    loop(2, project_q_own)
+    loads[4].wait()
+    loads[5].wait()
+    loop(2, project_do_own)
+    push_k.wait_recv()
     loop(4, turn)
+    push_x.wait_recv()
+    project_q(0, away)
+    push_dy.wait_recv()
+    project_do(0, away)
 
     def attend(h, j):
         n = (j + 1) * 256
@@ -381,7 +369,7 @@
     ring.drain()
     for c in stores:
         c.wait()
-    for c in (push_x, push_dy, push_kv, push_dx(0), push_dx(1)):
+    for c in (push_k, push_x, push_dy, push_kv, push_dx(0), push_dx(1)):
         c.wait_send()
     store_dx.wait()
 
@@ -402,7 +390,7 @@
             pltpu.VMEM((32, NH, E), F32), pltpu.VMEM((16, E), F32), pltpu.VMEM((16, E), F32), pltpu.VMEM((NH, 32, E), F32),
             bf(NT, 64, 32, 128), bf(NT, 16, 32, 128), bf(NT, 4, 32, 128),
             bf(NT, 3, 16, 32, 128), bf(NT, 3, 4, 32, 128), bf(NT, 3, 1, 32, 128),
-            dma((11,)), dma((5,)), dma((5,)), dma((len(GROUPS),)), dma((len(GROUPS), 3, 2))],
+            dma((11,)), dma((6,)), dma((6,)), dma((len(GROUPS),)), dma((len(GROUPS), 3, 2))],
         compiler_params=pltpu.CompilerParams(collective_id=0, has_side_effects=True, vmem_limit_bytes=67043328),
         cost_estimate=pl.CostEstimate(flops=3 * 10 ** 10, bytes_accessed=2 * 10 ** 7, transcendentals=0),
     )(x, dy, wq, wk, wv, wo)

time: 85.3 us -> 80.2 us (0.940)
  Pallas kernels: 84.3 us -> 79.3 us
    pallas_call x1, Pallas kernels: 81.7 us -> 76.7 us  [layer(): pl.pallas_call(layer_kernel, out_shape=(jax.ShapeDtypeStruct((HALF, D), B...]
where the time goes in v5:
time: 80.2 us; the launch traced here: 80.1 us
  Pallas kernels  79.3 us (99%)
    pallas_call x1, Pallas kernels, layer(): pl.pallas_call(layer_kernel, out_shape=(jax.ShapeDtypeStruct((HALF, D), B...  76.7 us
    pallas_call x1, Pallas kernels, hand_on(): pl.pallas_call(hand_on_kernel, out_shape=tuple((jax.ShapeDtypeStruct(a.sh...  2.58 us

profile of v5, /device:TPU:0, one launch (start us, length us, event | category | flops | bytes accessed | tf_op | source)
XLA Modules:
  0.0 80.1 jit_solution(10181709877999935919)
XLA Ops:
  0.6 76.7 %shard_map.101 = (bf16[512,2048]{1,0:T(8,128)(2,1)}, f32[32,4,256]{2,1,0:T(4,128)}, f32[16,256]{1,0:T(8,128)}, f32[16,256]{1,0:T(8,128)}, f32[4,32,256]{2,1,0:T(8,128)}) custom-call(bf16[512,2048]{1,0:T(8,128)(2,1)} %bitcast.8, bf16[512,2048]{1,0:T(8,128)(2,1)} %bitcast.9, bf16[2048,4,256]{2,1,0:T(4,128)(2,1)} %wq_hbm.1, bf16[2048,256]{1,0:T(8,128)(2,1)} %bitcast.11, ...), custom_call_target="tpu_custom_call" | custom-call | flops 30000001024 | bytes 20000000 | tf_op jit(solution)/shard_map/pallas_call | solution.py:381
  77.4 2.6 %shard_map.102 = (bf16[512,2048]{1,0:T(8,128)(2,1)}, f32[32,4,256]{2,1,0:T(4,128)}, f32[16,256]{1,0:T(8,128)}, f32[16,256]{1,0:T(8,128)}, f32[4,32,256]{2,1,0:T(8,128)}) custom-call(bf16[512,2048]{1,0:T(8,128)(2,1)} %get-tuple-element.15.dx, f32[32,4,256]{2,1,0:T(4,128)} %get-tuple-element.16.dwq, f32[16,256]{1,0:T(8,128)} %get-tuple-element.17.dwk, ...), custom_call_target="tpu_custom_call" | custom-call | flops 1000000 | bytes 6000000 | tf_op jit(solution)/shard_map/pallas_call | solution.py:415

commit v6 on v5

--- a/solution.py
+++ b/solution.py
@@ -10,7 +10,8 @@
 F32 = jnp.float32
 NT = 18
 SIZES = (16, 4, 1)
-GROUPS = ((0, 4), (4, 8), (8, 12), (12, 16), (16, 18))
+GROUPS = ((0, 4), (4, 8), (8, 12), (12, 14), (14, 16), (16, 18))
+COLOURS = (0, 1, 2, 0, 1, 2, 1, 0, 2)
 SEQ, HALF, D, E, NH = 1024, 512, 2048, 256, 4
 CD = E ** -0.5
 LOG2E = 1.4426950408889634
@@ -39,13 +40,8 @@
     return pl.ds(pl.multiple_of(i * size, size), size)
 
 
-def pick(i, a, b, c):
-    return a * ((1 - i) * (2 - i) // 2) + b * (i * (2 - i)) + c * (i * (i - 1) // 2)
-
-
 def steps_of(t):
-    k = (t // 2) % 3
-    return pick(k, 16, 1, 4), pick(k, 4, 16, 1), pick(k, 1, 4, 16)
+    return ((16, 4, 1), (1, 16, 4), (4, 1, 16))[COLOURS[t // 2]]
 
 
 class Ring:
@@ -61,11 +57,11 @@
                 pl.semaphore_signal(sem, inc=1, device_id={'data': self.at[ax][k][1]}, device_id_type=MESH)
 
     def ways(self, t, p):
-        ring = self.at[((t // 2) % 3 + p) % 3]
+        ring = self.at[(COLOURS[t // 2] + p) % 3]
         return (ring[0], ring[2], ring[1], ring[3]) if t % 2 == 0 else (ring[0], ring[2], ring[3], ring[1])
 
     def direct(self, g, p):
-        return p == 2 or (p == 1 and g >= 3)
+        return p == 2 or (p == 1 and g >= 2)
 
     def msg(self, g, t, p, n):
         _, opp, fwd, back = self.ways(t, p)
@@ -258,10 +254,10 @@
             for b, stages in enumerate(todo):
                 if 0 <= tick - 2 * b < 5:
                     next(stages)
-            if tick == 1:
-                project_q((h + 1) % NH, away)
-            if tick == 5:
-                project_do((h + 1) % NH, away)
+            if tick == 1 and h + 1 < NH:
+                project_q(h + 1, away)
+            if tick == 5 and h + 1 < NH:
+                project_do(h + 1, away)
 
     def store_tiles(t, v, i):
         sx, sy, sz = steps_of(t)
@@ -271,40 +267,53 @@
             for u in range(2):
                 b0[t + u, at] = v[j * 32:(j + 1) * 32, u * 128:(u + 1) * 128]
 
-    def weight_grads(h, i):
-        vo = nn(ot[...], dy[:, block(i, 512)]).astype(BF16).T
-        vq = nn(dqt[...], x[:, block(i, 512)]).astype(BF16).T
+    def tiles_of(lhs, rhs, i):
+        return nn(lhs[...], rhs[:, block(i, 512)]).astype(BF16).T
+
+    def store_block(t, v, i):
         for u in range(2):
-            store_tiles(h * 4, vo[u * 256:(u + 1) * 256], i * 2 + u)
-            store_tiles(h * 4 + 2, vq[u * 256:(u + 1) * 256], i * 2 + u)
+            store_tiles(t, v[u * 256:(u + 1) * 256], i * 2 + u)
+
+    def grads_two(lhs, rhs, t, i):
+        v = [tiles_of(lhs, rhs, i * 2 + u) for u in range(2)]
+        for u in range(2):
+            store_block(t, v[u], i * 2 + u)
     push_kv = push(dkv, dkv_in, 2)
-
-    def head_step(h):
+    for h in range(NH - 1):
         attention(h)
-
-        @pl.when(h == NH - 1)
-        def _():
-            push_kv.start()
-            ring.middle(0, 1)
+        if h == 2:
+            ring.finish(0, 0)
 
         def grads_step(i):
-            weight_grads(h, i)
-
-            def at(hh, ii, f):
-                @pl.when((h == hh) & (i == ii))
+            vo = tiles_of(ot, dy, i)
+            vq = tiles_of(dqt, x, i)
+            store_block(h * 4, vo, i)
+            store_block(h * 4 + 2, vq, i)
+            if h > 0:
+                @pl.when(i == 1)
                 def _():
-                    f()
-            for hh in range(2, NH):
-                at(hh, 0, lambda: ring.finish(hh - 2, 0))
-            for hh in range(1, NH):
-                at(hh, 2, lambda: ring.middle(hh - 1, 0))
-            for hh in range(NH):
-                at(hh, 3, lambda: ring.start(hh))
+                    ring.middle(h - 1, 0)
         loop(4, grads_step)
-    loop(NH, head_step)
-    ring.finish(0, 1)
+        ring.start(h)
+    attention(NH - 1)
+    push_kv.start()
+    ring.middle(0, 1)
+    ring.finish(1, 0)
+    loop(2, lambda i: grads_two(ot, dy, NH * 4 - 4, i))
+    ring.start(3)
+    loop(1, lambda i: grads_two(dqt, x, NH * 4 - 2, i))
+    ring.middle(2, 0)
+    loop(2, lambda i: grads_two(dqt, x, NH * 4 - 2, i), 1)
     ring.middle(1, 1)
-
+    ring.start(4)
+
+    def dx_away(i):
+        cols = block(i, 512)
+        wo[0:HALF, cols] = nt(dq[away], wq[cols]).astype(BF16)
+    def push_dx(i):
+        cols = pl.ds(i * 1024, 1024)
+        return push(wo.at[pl.ds(0, HALF), cols], dx_in.at[:, cols], 3 + i)
+    loop(1, dx_away)
     push_kv.wait_recv()
 
     def kv_sum(i):
@@ -323,23 +332,16 @@
                 b0[16 + u, at, 0:16] = rows[:, u * E:u * E + 128]
                 b0[16 + u, at, 16:32] = rows[:, u * E + 128:u * E + 256]
     loop(4, kv_block)
-    ring.start(4)
-
-    def dx_away(i):
-        cols = block(i, 512)
-        wo[0:HALF, cols] = nt(dq[away], wq[cols]).astype(BF16)
-    def push_dx(i):
-        cols = pl.ds(i * 1024, 1024)
-        return push(wo.at[pl.ds(0, HALF), cols], dx_in.at[:, cols], 3 + i)
-    loop(2, dx_away)
+    ring.start(5)
+    ring.finish(0, 1)
+
+    loop(2, dx_away, 1)
     push_dx(0).start()
-    ring.middle(3, 0)
-    ring.finish(2, 0)
     loop(4, dx_away, 2)
     push_dx(1).start()
-    ring.middle(4, 0)
-    ring.finish(1, 1)
-    ring.finish(0, 2)
+    for g in (3, 4, 5):
+        ring.middle(g, 0)
+    ring.finish(2, 0)
 
     def dx_own(i):
         cols = block(i, 512)
@@ -347,25 +349,31 @@
         wo[HALF:SEQ, cols] = (v + dx_in[:, cols].astype(F32)).astype(BF16)
     push_dx(0).wait_recv()
     loop(1, dx_own)
-    ring.middle(2, 1)
-    ring.finish(3, 0)
+    ring.finish(0, 2)
     loop(2, dx_own, 1)
-    ring.finish(4, 0)
+    ring.finish(1, 1)
     push_dx(1).wait_recv()
     loop(3, dx_own, 2)
-    ring.finish(2, 1)
-    ring.finish(1, 2)
+    ring.finish(4, 0)
+    ring.finish(3, 0)
     loop(4, dx_own, 3)
     store_dx = load(wo.at[pl.ds(HALF, HALF)], dx_hbm, 6)
     store_dx.start()
+    ring.finish(5, 0)
+    ring.finish(2, 1)
+    ring.finish(1, 2)
+    ring.finish(4, 1)
     ring.finish(3, 1)
-    ring.finish(4, 1)
-    for g in (2, 3, 4):
+    ring.finish(5, 1)
+    for g in (2, 4, 3):
         ring.finish(g, 2)
     stores = [load(a, b, 7 + i) for i, (a, b) in enumerate(
-        ((dwq_out, dwq_hbm), (dwk_out, dwk_hbm), (dwv_out, dwv_hbm), (dwo_out, dwo_hbm)))]
-    for c in stores:
-        c.start()
+        ((dwq_out, dwq_hbm), (dwo_out, dwo_hbm), (dwk_out, dwk_hbm), (dwv_out, dwv_hbm)))]
+    stores[0].start()
+    stores[1].start()
+    ring.finish(5, 2)
+    stores[2].start()
+    stores[3].start()
     ring.drain()
     for c in stores:
         c.wait()

time: 80.2 us -> 79.8 us (level)
  no operation moved by 1% of the time
where the time goes in v6:
time: 79.8 us; the launch traced here: 79.6 us
  Pallas kernels  78.8 us (99%)
  between operations  0.82 us (1%)
    pallas_call x1, Pallas kernels, layer(): pl.pallas_call(layer_kernel, out_shape=(jax.ShapeDtypeStruct((HALF, D), B...  76.2 us
    pallas_call x1, Pallas kernels, hand_on(): pl.pallas_call(hand_on_kernel, out_shape=tuple((jax.ShapeDtypeStruct(a.sh...  2.58 us

profile of v6, /device:TPU:0, one launch (start us, length us, event | category | flops | bytes accessed | tf_op | source)
XLA Modules:
  0.0 79.6 jit_solution(13428441962706758276)
XLA Ops:
  0.6 76.2 %shard_map.101 = (bf16[512,2048]{1,0:T(8,128)(2,1)}, f32[32,4,256]{2,1,0:T(4,128)}, f32[16,256]{1,0:T(8,128)}, f32[16,256]{1,0:T(8,128)}, f32[4,32,256]{2,1,0:T(8,128)}) custom-call(bf16[512,2048]{1,0:T(8,128)(2,1)} %bitcast.8, bf16[512,2048]{1,0:T(8,128)(2,1)} %bitcast.9, bf16[2048,4,256]{2,1,0:T(4,128)(2,1)} %wq_hbm.1, bf16[2048,256]{1,0:T(8,128)(2,1)} %bitcast.11, ...), custom_call_target="tpu_custom_call" | custom-call | flops 30000001024 | bytes 20000000 | tf_op jit(solution)/shard_map/pallas_call | solution.py:389
  76.8 2.6 %shard_map.102 = (bf16[512,2048]{1,0:T(8,128)(2,1)}, f32[32,4,256]{2,1,0:T(4,128)}, f32[16,256]{1,0:T(8,128)}, f32[16,256]{1,0:T(8,128)}, f32[4,32,256]{2,1,0:T(8,128)}) custom-call(bf16[512,2048]{1,0:T(8,128)(2,1)} %get-tuple-element.15.dx, f32[32,4,256]{2,1,0:T(4,128)} %get-tuple-element.16.dwq, f32[16,256]{1,0:T(8,128)} %get-tuple-element.17.dwk, ...), custom_call_target="tpu_custom_call" | custom-call | flops 1000000 | bytes 6000000 | tf_op jit(solution)/shard_map/pallas_call | solution.py:423

commit v7 on v6

--- a/solution.py
+++ b/solution.py
@@ -61,7 +61,7 @@
         return (ring[0], ring[2], ring[1], ring[3]) if t % 2 == 0 else (ring[0], ring[2], ring[3], ring[1])
 
     def direct(self, g, p):
-        return p == 2 or (p == 1 and g >= 2)
+        return p == 2 or (p == 1 and g >= 3)
 
     def msg(self, g, t, p, n):
         _, opp, fwd, back = self.ways(t, p)
@@ -313,7 +313,6 @@
     def push_dx(i):
         cols = pl.ds(i * 1024, 1024)
         return push(wo.at[pl.ds(0, HALF), cols], dx_in.at[:, cols], 3 + i)
-    loop(1, dx_away)
     push_kv.wait_recv()
 
     def kv_sum(i):
@@ -335,37 +334,38 @@
     ring.start(5)
     ring.finish(0, 1)
 
-    loop(2, dx_away, 1)
+    loop(2, dx_away)
     push_dx(0).start()
     loop(4, dx_away, 2)
     push_dx(1).start()
-    for g in (3, 4, 5):
-        ring.middle(g, 0)
-    ring.finish(2, 0)
+    ring.middle(3, 0)
+    ring.middle(4, 0)
+    ring.middle(5, 0)
 
     def dx_own(i):
         cols = block(i, 512)
         v = nt(dq[own], wq[cols]) + nt(dkvb[own], wkv[cols])
         wo[HALF:SEQ, cols] = (v + dx_in[:, cols].astype(F32)).astype(BF16)
     push_dx(0).wait_recv()
-    loop(1, dx_own)
-    ring.finish(0, 2)
-    loop(2, dx_own, 1)
-    ring.finish(1, 1)
+    loop(2, dx_own)
+    ring.finish(2, 0)
     push_dx(1).wait_recv()
     loop(3, dx_own, 2)
-    ring.finish(4, 0)
-    ring.finish(3, 0)
+    ring.finish(0, 2)
+    ring.finish(1, 1)
     loop(4, dx_own, 3)
     store_dx = load(wo.at[pl.ds(HALF, HALF)], dx_hbm, 6)
     store_dx.start()
+    ring.finish(4, 0)
+    ring.finish(3, 0)
     ring.finish(5, 0)
-    ring.finish(2, 1)
+    ring.middle(2, 1)
     ring.finish(1, 2)
     ring.finish(4, 1)
     ring.finish(3, 1)
     ring.finish(5, 1)
-    for g in (2, 4, 3):
+    ring.finish(2, 1)
+    for g in (4, 3, 2):
         ring.finish(g, 2)
     stores = [load(a, b, 7 + i) for i, (a, b) in enumerate(
         ((dwq_out, dwq_hbm), (dwo_out, dwo_hbm), (dwk_out, dwk_hbm), (dwv_out, dwv_hbm)))]

time: 79.8 us -> 78 us (0.977)
  Pallas kernels: 78.8 us -> 77.1 us
    pallas_call x1, Pallas kernels: 76.2 us -> 74.5 us  [layer(): pl.pallas_call(layer_kernel, out_shape=(jax.ShapeDtypeStruct((HALF, D), B...]
where the time goes in v7:
time: 78 us; the launch traced here: 77.9 us
  Pallas kernels  77.1 us (99%)
  between operations  0.82 us (1%)
    pallas_call x1, Pallas kernels, layer(): pl.pallas_call(layer_kernel, out_shape=(jax.ShapeDtypeStruct((HALF, D), B...  74.5 us
    pallas_call x1, Pallas kernels, hand_on(): pl.pallas_call(hand_on_kernel, out_shape=tuple((jax.ShapeDtypeStruct(a.sh...  2.58 us

profile of v7, /device:TPU:0, one launch (start us, length us, event | category | flops | bytes accessed | tf_op | source)
XLA Modules:
  0.0 77.9 jit_solution(8485133691408150574)
XLA Ops:
  0.6 74.5 %shard_map.101 = (bf16[512,2048]{1,0:T(8,128)(2,1)}, f32[32,4,256]{2,1,0:T(4,128)}, f32[16,256]{1,0:T(8,128)}, f32[16,256]{1,0:T(8,128)}, f32[4,32,256]{2,1,0:T(8,128)}) custom-call(bf16[512,2048]{1,0:T(8,128)(2,1)} %bitcast.8, bf16[512,2048]{1,0:T(8,128)(2,1)} %bitcast.9, bf16[2048,4,256]{2,1,0:T(4,128)(2,1)} %wq_hbm.1, bf16[2048,256]{1,0:T(8,128)(2,1)} %bitcast.11, ...), custom_call_target="tpu_custom_call" | custom-call | flops 30000001024 | bytes 20000000 | tf_op jit(solution)/shard_map/pallas_call | solution.py:389
  75.1 2.6 %shard_map.102 = (bf16[512,2048]{1,0:T(8,128)(2,1)}, f32[32,4,256]{2,1,0:T(4,128)}, f32[16,256]{1,0:T(8,128)}, f32[16,256]{1,0:T(8,128)}, f32[4,32,256]{2,1,0:T(8,128)}) custom-call(bf16[512,2048]{1,0:T(8,128)(2,1)} %get-tuple-element.15.dx, f32[32,4,256]{2,1,0:T(4,128)} %get-tuple-element.16.dwq, f32[16,256]{1,0:T(8,128)} %get-tuple-element.17.dwk, ...), custom_call_target="tpu_custom_call" | custom-call | flops 1000000 | bytes 6000000 | tf_op jit(solution)/shard_map/pallas_call | solution.py:423
